TPU v7x, 128 devices: a whole 4x4x4 slice. The times are simulated.
128 devices in a mesh: member: 16 (over z, x_lo, core), space: 8 (over x_hi, y).
Axes of the slice: x: 4 (x_hi: 2, x_lo: 2; x = x_hi * 2 + x_lo), y: 4, z: 4, core: 2. Of those that a mesh axis runs over, the one named last changes fastest.
Arguments:
- weather: bfloat16 [16, 84, 256, 1440], P('member', None, 'space'), may hold values from -6 to 6
- coefficients: int32 [16, 84, 2, 368, 361], P('member', None, None, 'space'), may hold values from -1073741824 to 1073741823
- channel_scale: float32 [84], replicated, may hold values from 0.3 to 3
Outputs:
- perturbed: bfloat16 [16, 84, 256, 1440], P('member', None, 'space')
All inputs are finite; a program needn't handle non-finite values.
Results may differ from a plain program's by a relative error of at most 0.007.
Values may be sent and summed in bfloat16 or wider, within the bound.
A program may use at most 192 MiB of HBM per device.

v0:
```python
import math

import jax
import jax.numpy as jnp
from jax import lax
from jax.sharding import PartitionSpec as P


def in_blocks(array, dim, devices):
    lengths = array.shape
    parts = array.reshape(*lengths[:dim], devices, lengths[dim] // devices, *lengths[dim + 1 :])
    return jnp.moveaxis(parts, dim, 0)


def joined_along(parts, dim):
    lengths = list(parts.shape[1:])
    lengths[dim] *= parts.shape[0]
    return jnp.moveaxis(parts, 0, dim).reshape(lengths)


def exchange_both(array, axis, axes, splits, concats):
    sizes = [lax.axis_size(a) for a in axes]
    parts = in_blocks(array, splits[0], sizes[0])
    parts = jnp.moveaxis(in_blocks(parts, splits[1] + 1, sizes[1]), 0, 1)
    inside = parts.shape[2:]
    parts = parts.reshape(-1, *inside)
    parts = lax.all_to_all(parts, axis, split_axis=0, concat_axis=0, tiled=True)
    parts = joined_along(parts.reshape(*sizes, *inside), concats[0] + 1)
    return joined_along(parts, concats[1])


def diagonal_log(order_count):
    steps_up = jnp.arange(1, order_count, dtype=jnp.int32).astype(jnp.float32)
    terms = 0.5 * jnp.log((2.0 * steps_up + 1.0) / (2.0 * steps_up))
    return jnp.concatenate([jnp.zeros((1,), jnp.float32), jnp.cumsum(terms)])


def legendre_table(orders, colatitude, order_logs, degree_count):
    order_values = orders.astype(jnp.float32)[:, None]
    cosine = jnp.cos(colatitude)[None, :]
    sine_values = jnp.sin(colatitude)[None, :]
    diagonal = jnp.exp(
        order_logs[:, None] - 0.5 * math.log(4.0 * math.pi) + order_values * jnp.log(sine_values)
    )
    block_size = 16
    turn_count = (degree_count + block_size - 1) // block_size
    order_square = order_values * order_values

    def advance(carry, turn_index):
        older_row, newer_row = carry
        produced = []
        for inner_step in range(block_size):
            degree = (turn_index * block_size + inner_step).astype(jnp.float32)
            degree_square = degree * degree
            prior = degree - 1.0
            factor_up = jnp.sqrt(
                jnp.maximum(4.0 * degree_square - 1.0, 1.0)
                / jnp.maximum(degree_square - order_square, 1.0)
            )
            factor_down = jnp.sqrt(
                jnp.maximum(prior * prior - order_square, 0.0)
                / jnp.maximum(4.0 * prior * prior - 1.0, 1.0)
            )
            next_row = factor_up * (cosine * newer_row - factor_down * older_row)
            next_row = jnp.where(
                degree < order_values, 0.0, jnp.where(degree == order_values, diagonal, next_row)
            )
            produced.append(next_row)
            older_row, newer_row = (newer_row, next_row)
        return ((older_row, newer_row), jnp.stack(produced))

    empty = jnp.zeros_like(diagonal)
    carried, stacked = lax.scan(advance, (empty, empty), jnp.arange(turn_count, dtype=jnp.int32))
    return stacked.reshape(turn_count * block_size, orders.shape[0], colatitude.shape[0])[
        :degree_count
    ]


def spectral_values(coefficients, orders):
    degree_count = coefficients.shape[-1]
    degrees = jnp.arange(degree_count, dtype=jnp.int32)
    keep = degrees[None, :] >= orders[:, None]
    factor = math.sqrt(3.0) * math.sqrt(4.0 * math.pi) / degree_count * 2.0 ** (-30)
    values = coefficients.astype(jnp.float32) * factor
    return jnp.where(keep, values, 0.0).astype(jnp.bfloat16)


def fourier_basis(order_count, lon_count):
    orders = jnp.arange(order_count, dtype=jnp.int32)
    columns = jnp.arange(lon_count, dtype=jnp.int32)
    phases = orders[:, None] * columns[None, :] % lon_count
    angles = 2.0 * math.pi / lon_count * phases.astype(jnp.float32)
    weights = jnp.where(orders == 0, 1.0, math.sqrt(2.0)).astype(jnp.float32)[:, None]
    return jnp.stack([weights * jnp.cos(angles), weights * jnp.sin(angles)]).astype(jnp.bfloat16)


def local(weather, coefficients, channel_scale):
    group_count = lax.axis_size("member")
    band_count = lax.axis_size("space")
    member_local, channels, rows_local, lon_count = weather.shape
    order_local = coefficients.shape[3]
    degree_count = coefficients.shape[4]
    order_count = order_local * band_count
    lat_count = rows_local * band_count
    lat_local = rows_local // group_count
    member_count = member_local * group_count
    first_order = lax.axis_index("space") * order_local
    orders = first_order + jnp.arange(order_local, dtype=jnp.int32)
    order_logs = lax.dynamic_slice_in_dim(diagonal_log(order_count), first_order, order_local)
    row_first = (lon_count // 2 + 1 - lat_count) // 2
    colatitude = (
        math.pi
        * (row_first + jnp.arange(lat_count, dtype=jnp.int32)).astype(jnp.float32)
        / (lon_count // 2)
    )
    legendre = legendre_table(orders, colatitude, order_logs, degree_count).astype(jnp.bfloat16)
    spectral = spectral_values(coefficients, orders)
    fourier = jnp.einsum(
        "ecpml,lmt->ectpm", spectral, legendre, preferred_element_type=jnp.float32
    ).astype(jnp.bfloat16)
    fourier = fourier.reshape(
        member_local, channels, band_count, group_count, lat_local, 2, order_local
    )
    basis = fourier_basis(order_count, lon_count).reshape(2 * order_count, lon_count)
    scale_wide = channel_scale[None, :, None, None, None]
    pieces = weather.reshape(member_local, channels, group_count, lat_local, lon_count)
    banded = exchange_both(fourier, ("member", "space"), ("member", "space"), (3, 2), (0, 6))
    fourier_rows = banded.reshape(member_count * channels * lat_local, 2 * order_count)
    noise = jnp.dot(fourier_rows, basis, preferred_element_type=jnp.float32).astype(jnp.bfloat16)
    noise = noise.reshape(member_count, channels, 1, lat_local, lon_count)
    noise_wide = lax.optimization_barrier(noise).astype(jnp.float32)
    band_mean = jnp.sum(noise_wide, axis=0, keepdims=True) / member_count
    weather_bands = lax.all_to_all(pieces, "member", split_axis=2, concat_axis=0, tiled=True)
    perturbed = (weather_bands.astype(jnp.float32) + scale_wide * (noise_wide - band_mean)).astype(
        jnp.bfloat16
    )
    returned = lax.all_to_all(perturbed, "member", split_axis=0, concat_axis=2, tiled=True)
    return returned.reshape(member_local, channels, rows_local, lon_count)


def solution(mesh):
    return jax.shard_map(
        local,
        mesh=mesh,
        in_specs=(P("member", None, "space", None), P("member", None, None, "space", None), P()),
        out_specs=P("member", None, "space", None),
        check_vma=False,
    )
```

profile of v0, /device:TPU:1, one launch (start us, length us, event | category | flops | bytes accessed | tf_op | source)
XLA Modules:
  0.0 521.1 jit_solution(6489075889256272937)
XLA Ops:
  0.9 127.6 %while.21 = (s32[]{:T(128)}, f32[46,256]{1,0:T(8,128)S(1)}, f32[46,256]{1,0:T(8,128)S(1)}, bf16[23,16,46,256]{3,2,1,0:T(8,128)(2,1)}, s32[23]{0:T(128)S(1)}, /*i...) while((s32[]{:T(128)}, f32[46,256]{1,0:T(8,128)S(1)}, ...), condition=%wide.region_3.4_spmd.clone.clone.clone.clone, body=%wide.region_2.3_spmd.clone.clone.clone.clone.sunk | while | flops 3519778 | bytes 3859869 | solution.py:73
  0.9 0.6 dynamic_slice.18
  5.7 0.8 bitcast_dynamic-update-slice_fusion.50
  6.4 0.6 dynamic_slice.18
  11.2 0.8 bitcast_dynamic-update-slice_fusion.50
  16.7 0.8 bitcast_dynamic-update-slice_fusion.50
  22.3 0.8 bitcast_dynamic-update-slice_fusion.50
  27.8 0.8 bitcast_dynamic-update-slice_fusion.50
  33.3 0.8 bitcast_dynamic-update-slice_fusion.50
  38.9 0.8 bitcast_dynamic-update-slice_fusion.50
  44.4 0.8 bitcast_dynamic-update-slice_fusion.50
  50.0 0.8 bitcast_dynamic-update-slice_fusion.50
  55.5 0.8 bitcast_dynamic-update-slice_fusion.50
  61.0 0.8 bitcast_dynamic-update-slice_fusion.50
  66.6 0.8 bitcast_dynamic-update-slice_fusion.50
  72.1 0.8 bitcast_dynamic-update-slice_fusion.50
  77.7 0.8 bitcast_dynamic-update-slice_fusion.50
  83.2 0.8 bitcast_dynamic-update-slice_fusion.50
  88.7 0.8 bitcast_dynamic-update-slice_fusion.50
  94.3 0.8 bitcast_dynamic-update-slice_fusion.50
  99.8 0.8 bitcast_dynamic-update-slice_fusion.50
  105.4 0.8 bitcast_dynamic-update-slice_fusion.50
  110.9 0.8 bitcast_dynamic-update-slice_fusion.50
  116.5 0.8 bitcast_dynamic-update-slice_fusion.50
  122.1 0.8 bitcast_dynamic-update-slice_fusion.50
  127.7 0.8 bitcast_dynamic-update-slice_fusion.50
  128.5 10.1 %copy.39 = bf16[23,16,46,256]{3,1,0,2:T(8,128)(2,1)} copy(bf16[23,16,46,256]{3,2,1,0:T(8,128)(2,1)} %get-tuple-element.233) | data formatting | bytes 17334272 | tf_op jit(solution)/shard_map/convert.6
  138.6 11.3 %fusion.48 = bf16[84,2,46,361]{3,1,2,0:T(2,128)(2,1)} fusion(s32[1,84,2,46,361]{4,2,3,1,0:T(2,128)} %param.6, pred[46,361]{1,0:T(8,128)(4,1)S(1)} %iota_compare_fusion), kind=kLoop, calls=%fused_computation.136 | loop fusion | flops 11159232 | bytes 16755454 | tf_op jit(solution)/shard_map/reshape.8
  149.9 6.9 %convert_bitcast_fusion = bf16[1,84,256,2,46]{2,1,3,4,0:T(8,128)(2,1)} fusion(bf16[84,2,46,361]{3,1,2,0:T(2,128)(2,1)} %fusion.48, bf16[368,46,256]{2,0,1:T(8,128)(2,1)S(1)} %bitcast.379), kind=kOutput, calls=%fused_computation.137 | convolution fusion | flops 1430360064 | bytes 18203488 | tf_op jit(solution)/shard_map/ecpml,lmt->ectpm/dot_general | solution.py:118
  156.8 7.8 %copy.41 = bf16[1,84,256,2,46]{1,2,4,3,0:T(8,128)(2,1)} copy(bf16[1,84,256,2,46]{2,1,3,4,0:T(8,128)(2,1)} %convert_bitcast_fusion) | data formatting | bytes 7913472 | tf_op jit(solution)/shard_map/convert_element_type | solution.py:120
  164.7 5.7 %copy.55 = bf16[16,8,1,84,1,1,2,2,46]{3,1,0,8,7,6,5,4,2:T(8,128)(2,1)S(1)} copy(bf16[16,8,1,84,1,1,2,2,46]{3,6,0,1,8,7,5,4,2:T(2,128)(2,1)} %bitcast.377) | data formatting | bytes 7913472 | tf_op jit(solution)/shard_map/transpose;transpose | solution.py:24
  170.4 27.3 %copy.43 = bf16[128,1,84,1,1,2,2,46]{2,6,7,5,4,3,1,0:T(2,128)(2,1)} copy(bf16[128,1,84,1,1,2,2,46]{2,0,7,6,5,4,3,1:T(8,128)(2,1)S(1)} %bitcast.378) | data formatting | bytes 7913472 | tf_op jit(solution)/shard_map/reshape | solution.py:26
  197.7 11.9 %all-to-all-start.1 = ((bf16[128,1,84,1,1,2,2,46]{2,6,7,5,4,3,1,0:T(2,128)(2,1)}), bf16[128,1,84,1,1,2,2,46]{2,6,7,5,4,3,1,0:T(2,128)(2,1)}, u32[]{:S(2)}, u32[]{:S(2)}) async-start(bf16[128,1,84,1,1,2,2,46]{2,6,7,5,4,3,1,0:T(2,128)(2,1)} %copy.43), calls=%async_computation.1 | async-start | bytes 12058624 | tf_op jit(solution)/shard_map/all_to_all | solution.py:27
  209.6 11.3 %copy.36 = bf16[1,84,32,1440]{3,1,2,0:T(8,128)(2,1)} copy(bf16[1,84,32,1440]{3,2,1,0:T(8,128)(2,1)} %param.5) | data formatting | bytes 15482880 | tf_op args[0]
  220.9 12.9 %copy.37 = bf16[1,84,16,2,1440]{4,3,1,0,2:T(2,128)(2,1)} copy(bf16[1,84,16,2,1440]{4,1,3,2,0:T(8,128)(2,1)} %bitcast.375) | data formatting | bytes 15482880 | tf_op jit(solution)/shard_map/reshape | solution.py:126
  233.8 45.8 %all-to-all-done.1 = bf16[128,1,84,1,1,2,2,46]{2,6,7,5,4,3,1,0:T(2,128)(2,1)} async-done(((bf16[128,1,84,1,1,2,2,46]{2,6,7,5,4,3,1,0:T(2,128)(2,1)}), bf16[128,1,84,1,1,2,2,46]{2,6,7,5,4,3,1,0:T(2,128)(2,1)}, u32[]{:S(2)}, u32[]{:S(2)}) %all-to-all-start.1) | async-done | bytes 3956768 | tf_op jit(solution)/shard_map/all_to_all | solution.py:27
  279.6 9.2 %all-to-all-start = ((bf16[1,84,16,2,1440]{4,3,1,0,2:T(2,128)(2,1)}), bf16[1,84,16,2,1440]{4,3,1,0,2:T(2,128)(2,1)}, u32[]{:S(2)}, u32[]{:S(2)}) async-start(bf16[1,84,16,2,1440]{4,3,1,0,2:T(2,128)(2,1)} %copy.37), calls=%async_computation | async-start | bytes 16515072 | tf_op jit(solution)/shard_map/all_to_all | solution.py:133
  288.8 9.8 %multiply_convert_fusion.1 = (bf16[1,368,1440]{2,1,0:T(8,128)(2,1)S(1)}, bf16[1,368,1440]{2,1,0:T(8,128)(2,1)S(1)}) fusion(f32[368]{0:T(512)S(1)} %fusion.58), kind=kLoop, calls=%fused_computation.143 | loop fusion | flops 6888960 | bytes 2121152 | tf_op jit(solution)/shard_map/convert.3
  298.8 24.1 %copy.44 = bf16[16,8,1,84,1,1,2,2,46]{8,1,7,6,3,0,5,4,2:T(8,128)(2,1)} copy(bf16[16,8,1,84,1,1,2,2,46]{3,7,8,6,1,0,5,4,2:T(2,128)(2,1)} %bitcast.18) | data formatting | bytes 7913472 | tf_op jit(solution)/shard_map/reshape | solution.py:28
  322.9 16.2 %reshape_reshape.7 = bf16[2688,736]{1,0:T(8,128)(2,1)} reshape(bf16[16,84,1,1,2,2,8,46]{7,6,5,4,1,0,3,2:T(8,128)(2,1)} %bitcast.373) | data formatting | bytes 7913472 | tf_op jit(solution)/shard_map/reshape;reshape | solution.py:128
  339.1 11.2 %convolution_convert_fusion = bf16[2688,1440]{0,1:T(8,128)(2,1)} fusion(bf16[2688,736]{1,0:T(8,128)(2,1)} %reshape_reshape.7, bf16[736,1440]{1,0:T(8,128)(2,1)S(1)} %bitcast.396), kind=kOutput, calls=%fused_computation.130 | convolution fusion | flops 5701570560 | bytes 13817856 | tf_op jit(solution)/shard_map/dot_general | solution.py:129
  350.3 11.6 %copy.45 = bf16[2688,1440]{1,0:T(8,128)(2,1)} copy(bf16[2688,1440]{0,1:T(8,128)(2,1)} %convolution_convert_fusion) | data formatting | bytes 15482880 | tf_op jit(solution)/shard_map/convert_element_type | solution.py:129
  361.9 17.0 %reshape.1212 = bf16[16,84,1,2,1440]{4,3,1,0,2:T(2,128)(2,1)} reshape(bf16[2688,1440]{1,0:T(8,128)(2,1)} %copy.45) | data formatting | bytes 15482880 | tf_op jit(solution)/shard_map/reshape | solution.py:130
  378.9 9.6 %convert_reduce_fusion = f32[84,2,1440]{2,1,0:T(2,128)S(1)} fusion(bf16[16,84,1,2,1440]{4,3,1,0,2:T(2,128)(2,1)} %reshape.1212), kind=kLoop, calls=%fused_computation.125 | loop fusion | flops 7499520 | bytes 8709120 | tf_op jit(solution)/shard_map/reduce_sum | solution.py:132
  389.0 15.5 %fusion.46 = bf16[16,84,1,2,1440]{4,3,2,1,0:T(2,128)(2,1)S(1)} fusion(f32[84,2,1440]{2,1,0:T(2,128)S(1)} %broadcast_multiply_fusion, bf16[16,84,1,2,1440]{4,3,1,0,2:T(2,128)(2,1)} %reshape.1212, f32[84]{0:T(128)S(1)} %copy-done.1, bf16[1,84,16,2,1440]{4,3,1,0,2:T(2,128)(2,1)} %all-to-all-done), kind=kLoop, calls=%fused_computation.133 | loop fusion | flops 23224320 | bytes 24192336 | tf_op jit(solution)/shard_map/convert_element_type | solution.py:134
  404.5 98.2 %all_to_all.29 = bf16[16,84,1,2,1440]{4,3,2,1,0:T(2,128)(2,1)} all-to-all(bf16[16,84,1,2,1440]{4,3,2,1,0:T(2,128)(2,1)S(1)} %fusion.46), channel_id=1, replica_groups=mesh['member'=16,'space'=8] {'member'}, dimensions={0} | all-to-all | bytes 15482880 | tf_op jit(solution)/shard_map/all_to_all | solution.py:137
  502.7 8.5 %copy.47 = bf16[1,84,16,1,2,1440]{5,1,4,2,3,0:T(8,128)(2,1)} copy(bf16[1,84,16,1,2,1440]{5,4,1,2,3,0:T(2,128)(2,1)} %bitcast.376) | data formatting | bytes 15482880 | tf_op jit(solution)/shard_map/all_to_all | solution.py:137
  511.1 9.5 %copy.48 = bf16[1,84,32,1440]{3,2,1,0:T(8,128)(2,1)} copy(bf16[1,84,32,1440]{3,1,2,0:T(8,128)(2,1)} %bitcast.374) | data formatting | bytes 15482880 | tf_op jit(solution)/shard_map/reshape | solution.py:138
  (1172 shorter events, 82.7 us)
Async XLA Ops:
  138.6 11.3 %copy-start = (bf16[23,16,46,256]{3,1,0,2:T(8,128)(2,1)S(1)}, bf16[23,16,46,256]{3,1,0,2:T(8,128)(2,1)}, u32[]{:S(2)}) copy-start(bf16[23,16,46,256]{3,1,0,2:T(8,128)(2,1)} %copy.39) | copy-start | bytes 26001412
  197.7 81.9 %all-to-all-start.1 = ((bf16[128,1,84,1,1,2,2,46]{2,6,7,5,4,3,1,0:T(2,128)(2,1)}), bf16[128,1,84,1,1,2,2,46]{2,6,7,5,4,3,1,0:T(2,128)(2,1)}, u32[]{:S(2)}, u32[]{:S(2)}) async-start(bf16[128,1,84,1,1,2,2,46]{2,6,7,5,4,3,1,0:T(2,128)(2,1)} %copy.43), calls=%async_computation.1 | async-start | bytes 12058624 | tf_op jit(solution)/shard_map/all_to_all | solution.py:27
  279.6 109.4 %all-to-all-start = ((bf16[1,84,16,2,1440]{4,3,1,0,2:T(2,128)(2,1)}), bf16[1,84,16,2,1440]{4,3,1,0,2:T(2,128)(2,1)}, u32[]{:S(2)}, u32[]{:S(2)}) async-start(bf16[1,84,16,2,1440]{4,3,1,0,2:T(2,128)(2,1)} %copy.37), calls=%async_computation | async-start | bytes 16515072 | tf_op jit(solution)/shard_map/all_to_all | solution.py:133
  378.9 10.1 %copy-start.1 = (f32[84]{0:T(128)S(1)}, f32[84]{0:T(128)}, u32[]{:S(2)}) copy-start(f32[84]{0:T(128)} %param.7) | copy-start | bytes 1012
where the time goes:
time: 530 us; the launch traced here: 521 us
  local copies, waits for them, and re-layouts  195 us (37%)
  other arithmetic  115 us (22%)
  blocking collectives  98.2 us (19%)
  waiting for transfers between devices  45.8 us (9%)
  loops' own time  27.1 us (5%)
  starting transfers between devices  21.1 us (4%)
  matrix products  18.1 us (3%)
    all_to_all x1, blocking collectives, local(): lax.all_to_all(perturbed, 'member', split_axis=0, concat_axis=2, tiled=True)  98.2 us
    while x345, other arithmetic  53.9 us
    all_to_all x1, waiting for transfers between devices, exchange_both(): parts = lax.all_to_all(parts, axis, split_axis=0, concat_axis=0, tiled=True)  45.8 us
    reshape x1, local copies, waits for them, and re-layouts, exchange_both(): parts = parts.reshape(-1, *inside)  27.3 us
    another operation x1, loops' own time, legendre_table(): lax.scan(advance, (empty, empty), jnp.arange(turn_count, dtype=jnp.int32))  27.1 us
    reshape x1, local copies, waits for them, and re-layouts, exchange_both(): parts = joined_along(parts.reshape(*sizes, *inside), concats[0] + 1)  24.1 us
    another operation x5, other arithmetic  21.5 us
    dynamic_update_slice x23, local copies, waits for them, and re-layouts, legendre_table(): lax.scan(advance, (empty, empty), jnp.arange(turn_count, dtype=jnp.int32))  18.2 us
  transfers between devices with their start and end apart: 2, of which 1 were waited for; matrix products, arithmetic and copies ran while one was open for 24% of the time, Pallas kernels for 0%

commit v1 on v0

v1 whole, which is shorter than its diff:
```python
import functools
import math

import jax
import jax.numpy as jnp
from jax import lax
from jax.experimental import pallas as pl
from jax.experimental.pallas import tpu as pltpu
from jax.sharding import PartitionSpec as P

MESH = pl.DeviceIdType.MESH

CH = 84
LON = 1440
TCOUNT = 256
LP = 361
BANDS = 8
ORDERS = 46
CHUNKS = 2
ORDP = 24
Q = 4
R = CH // Q
RP = 24
MROWS = 2 * Q * RP
MP = MROWS + 8
LROWS = 392
GROUP = 2 * ORDP
ROWS = CHUNKS * R * GROUP
ROWSP = 2048
OWN = 128
FACTOR = math.sqrt(3.0) * math.sqrt(4.0 * math.pi) / LP * 2.0 ** (-30)


def diagonal_log(order_count):
    steps_up = jnp.arange(1, order_count, dtype=jnp.int32).astype(jnp.float32)
    terms = 0.5 * jnp.log((2.0 * steps_up + 1.0) / (2.0 * steps_up))
    return jnp.concatenate([jnp.zeros((1,), jnp.float32), jnp.cumsum(terms)])


def lane_blocks(values, lane):
    low = lane < 64

    def swap(a, b, width, mask):
        ra = pltpu.roll(a, 128 - width, 1)
        rb = pltpu.roll(b, width, 1)
        return jnp.where(mask, a, rb), jnp.where(mask, ra, b)

    v0, v1, v2, v3 = values
    a0, a2 = swap(v0, v2, 64, low)
    a1, a3 = swap(v1, v3, 64, low)
    even = (lane % 64) < 32
    b0, b1 = swap(a0, a1, 32, even)
    b2, b3 = swap(a2, a3, 32, even)
    return b0, b1, b2, b3


def transform_kernel(coef_ref, cos_ref, diag_ref, f_ref, coef_v, lhs_v, tab, stage, sems):
    space = lax.axis_index("space")
    loads = [
        pltpu.make_async_copy(
            coef_ref.at[0, pl.ds(q * R, R)], coef_v.at[pl.ds(q * R, R)], sems.at[q]
        )
        for q in range(Q)
    ]
    for load in loads:
        load.start()

    def clear_lhs(n, _):
        lhs_v[2, pl.ds(pl.multiple_of(n * MP, 8), MP), :] = jnp.zeros((MP, 128), jnp.float32)
        return 0

    lax.fori_loop(0, ORDP, clear_lhs, 0)

    def clear_table(i, _):
        for h in range(2):
            for at in range(LP // 8 * 8, 384, 8):
                tab[h, pl.ds(pl.multiple_of(i * LROWS + at, 8), 8), :] = jnp.zeros(
                    (8, 128), jnp.float32
                )
        return 0

    lax.fori_loop(0, ORDP, clear_table, 0)

    def table(k):
        first = space * ORDERS + k * ORDP
        order = (first + lax.broadcasted_iota(jnp.int32, (ORDP, 128), 0)).astype(jnp.float32)
        square = order * order
        order_wide = first + lax.broadcasted_iota(jnp.int32, (ORDP, TCOUNT), 0)
        cosine = jnp.broadcast_to(cos_ref[...], (ORDP, TCOUNT))
        diag = diag_ref[k]
        older = jnp.zeros((ORDP, TCOUNT), jnp.float32)
        newer = jnp.zeros((ORDP, TCOUNT), jnp.float32)
        for tile in range(3):
            degree = tile * 128 + lax.broadcasted_iota(jnp.int32, (ORDP, 128), 1)
            degree = degree.astype(jnp.float32)
            degree_square = degree * degree
            prior = degree - 1.0
            up = jnp.sqrt(
                jnp.maximum(4.0 * degree_square - 1.0, 1.0)
                / jnp.maximum(degree_square - square, 1.0)
            )
            down = jnp.sqrt(
                jnp.maximum(prior * prior - square, 0.0)
                / jnp.maximum(4.0 * prior * prior - 1.0, 1.0)
            )

            def block(j, carry, steps=8):
                older, newer, up, down = carry
                for u in range(steps):
                    deg = tile * 128 + j * 8 + u
                    nxt = up[:, u : u + 1] * (cosine * newer - down[:, u : u + 1] * older)
                    nxt = jnp.where(order_wide == deg, diag, nxt)
                    for b in range(ORDP // 8):
                        for h in range(2):
                            tab[h, pl.ds(b * 8 * LROWS + deg, 8, stride=LROWS), :] = nxt[
                                8 * b : 8 * b + 8, 128 * h : 128 * h + 128
                            ]
                    older, newer = newer, nxt
                return older, newer, pltpu.roll(up, 120, 1), pltpu.roll(down, 120, 1)

            count = min(16, (LP - 128 * tile) // 8)
            carry = lax.fori_loop(0, count, block, (older, newer, up, down))
            if tile == 2:
                block(count, carry, steps=LP % 8)
            older, newer = carry[:2]

    def arrange(k, q):
        def one(r, _):
            for i in range(min(ORDP, ORDERS - k * ORDP)):
                for t in range(3):
                    wide = min(128, LP - 128 * t)
                    raw = coef_v[q * R + r, k * ORDP + i, :, pl.ds(128 * t, wide)]
                    lhs_v[t, pl.ds(i * MP + q * 48 + r, 2, stride=RP), pl.ds(0, wide)] = (
                        raw.astype(jnp.float32) * FACTOR
                    )
            return 0

        lax.fori_loop(0, R, one, 0)

    lane = lax.broadcasted_iota(jnp.int32, (RP * 2, 128), 1)

    def orders_of(k):
        def one(i, _):
            row = pl.multiple_of(i * MP, 8)
            lhs = jnp.concatenate(
                [lhs_v[t, pl.ds(row, MROWS), :].astype(jnp.bfloat16) for t in range(3)], axis=1
            )
            row = pl.multiple_of(i * LROWS, 8)
            rhs = jnp.concatenate(
                [tab[h, pl.ds(row, 384), :].astype(jnp.bfloat16) for h in range(2)], axis=1
            )
            out = jnp.dot(lhs, rhs, preferred_element_type=jnp.float32)
            for h in range(2):
                parts = [
                    out[48 * q : 48 * q + 48, 128 * h : 128 * h + 128] for q in range(Q)
                ]
                for b, part in enumerate(lane_blocks(parts, lane)):
                    s = 4 * h + b
                    for a in range(6):
                        stage[pl.ds((s * 48 + 8 * a) * ORDP + i, 8, stride=ORDP), :] = part[
                            8 * a : 8 * a + 8
                        ]
            return 0

        lax.fori_loop(0, min(ORDP, ORDERS - k * ORDP), one, 0)

    def pack_of(k):
        def pack(n, _):
            s, r = n // R, n % R
            first = stage[pl.ds(pl.multiple_of((s * 48 + r) * ORDP, 8), ORDP), :]
            second = stage[pl.ds(pl.multiple_of((s * 48 + RP + r) * ORDP, 8), ORDP), :]
            both = jnp.concatenate([first, second], axis=0).astype(jnp.bfloat16)
            f_ref[s, pl.ds(pl.multiple_of((k * R + r) * GROUP, 16), GROUP), :] = both
            return 0

        lax.fori_loop(0, BANDS * R, pack, 0)

    def clear(n, _):
        for i in range(ORDERS - ORDP, ORDP):
            stage[pl.ds(n * 8 * ORDP + i, 8, stride=ORDP), :] = jnp.zeros(
                (8, 128), jnp.float32
            )
        return 0

    for s in range(BANDS):
        f_ref[s, pl.ds(ROWS, ROWSP - ROWS), :] = jnp.zeros((ROWSP - ROWS, 128), jnp.bfloat16)

    table(0)
    for q in range(Q):
        loads[q].wait()
        arrange(0, q)
    orders_of(0)
    pack_of(0)
    lax.fori_loop(0, BANDS * 48 // 8, clear, 0)
    table(1)
    for q in range(Q):
        arrange(1, q)
    orders_of(1)
    pack_of(1)


def transform(coefficients, cosine, diag):
    return pl.pallas_call(
        transform_kernel,
        name="transform",
        out_shape=jax.ShapeDtypeStruct((BANDS, ROWSP, 128), jnp.bfloat16),
        in_specs=[
            pl.BlockSpec(memory_space=pl.ANY),
            pl.BlockSpec(memory_space=pltpu.VMEM),
            pl.BlockSpec(memory_space=pltpu.VMEM),
        ],
        out_specs=pl.BlockSpec(memory_space=pltpu.VMEM),
        scratch_shapes=[
            pltpu.VMEM((CH, ORDERS, 2, LP), jnp.int32),
            pltpu.VMEM((3, ORDP * MP, 128), jnp.float32),
            pltpu.VMEM((2, ORDP * LROWS, 128), jnp.float32),
            pltpu.VMEM((BANDS * 48 * ORDP, 128), jnp.float32),
            pltpu.SemaphoreType.DMA((Q,)),
        ],
        compiler_params=pltpu.CompilerParams(vmem_limit_bytes=56 * 2**20),
    )(coefficients, cosine, diag)


def exchange_kernel(
    f_ref, out_ref, basis_ref,
    got, mean, buf_a, buf_b, buf_c, piece,
    raw_s, raw_r, sa, ra, sb, rb, sc, rc, sd, rd, se, re, sf, rf, sg, rg,
):
    member, space = lax.axis_index("member"), lax.axis_index("space")
    z, xl, core = member // 4, (member // 2) % 2, member % 2

    def member_of(z, xl, core):
        return (z * 2 + xl) * 2 + core

    z_peers = [member_of((z + d) % 4, xl, core) for d in (1, 2, 3)]
    x_peer = member_of(z, 1 - xl, core)
    c_peer = member_of(z, xl, 1 - core)
    s_peers = [(space + d) % BANDS for d in range(1, BANDS)]
    barrier = pltpu.get_barrier_semaphore()
    for peer in z_peers + [x_peer, c_peer]:
        pl.semaphore_signal(barrier, inc=1, device_id=(peer, space), device_id_type=MESH)
    for peer in s_peers:
        pl.semaphore_signal(barrier, inc=1, device_id=(member, peer), device_id_type=MESH)
    pl.semaphore_wait(barrier, 5 + BANDS - 1)

    def remote(src, dst, ss, rs, device):
        return pltpu.make_async_remote_copy(
            src_ref=src, dst_ref=dst, send_sem=ss, recv_sem=rs,
            device_id=device, device_id_type=MESH,
        )

    half = 8 * OWN
    mine = pl.multiple_of(core * half, 16)
    other = pl.multiple_of((1 - core) * half, 16)
    pair = remote(f_ref.at[:, pl.ds(other, half)], buf_a, sa, ra, (c_peer, space))
    pair.start()
    raws = []
    for d in range(1, BANDS):
        raws.append(
            remote(
                f_ref.at[(space + d) % BANDS], got.at[d],
                raw_s.at[d - 1], raw_r.at[d - 1], (member, (space + d) % BANDS),
            )
        )
        raws[-1].start()

    pair.wait()

    def add_pair(n, _):
        s, j = n // 8, n % 8
        at = pl.multiple_of(j * 128, 16)
        total = buf_a[s, pl.ds(at, 128), :].astype(jnp.float32) + f_ref[
            s, pl.ds(mine + at, 128), :
        ].astype(jnp.float32)
        buf_a[s, pl.ds(at, 128), :] = total.astype(jnp.bfloat16)
        return 0

    lax.fori_loop(0, BANDS * 8, add_pair, 0)
    zs = []
    for d in (1, 2, 3):
        at = pl.multiple_of(((z + d) % 4) * 256, 16)
        zs.append(
            remote(
                buf_a.at[:, pl.ds(at, 256)], buf_b.at[d - 1],
                sb.at[d - 1], rb.at[d - 1], (z_peers[d - 1], space),
            )
        )
        zs[-1].start()

    column = lax.broadcasted_iota(jnp.int32, (ORDP, LON), 1).astype(jnp.float32)
    index = lax.broadcasted_iota(jnp.int32, (ORDP, LON), 0)

    def basis_block(n, _):
        order = n // CHUNKS * ORDERS + n % CHUNKS * ORDP + index
        product = order.astype(jnp.float32) * column
        turns = jnp.floor((product + 0.5) * (1.0 / LON))
        phase = product - turns * LON
        angle = 2.0 * math.pi / LON * phase
        weight = jnp.where(order == 0, 1.0, math.sqrt(2.0))
        weight = jnp.where(n % CHUNKS * ORDP + index < ORDERS, weight, 0.0)
        both = jnp.concatenate([weight * jnp.cos(angle), weight * jnp.sin(angle)], axis=0)
        basis_ref[pl.ds(pl.multiple_of(n * GROUP, 16), GROUP), :] = both.astype(jnp.bfloat16)
        return 0

    lax.fori_loop(0, BANDS * CHUNKS, basis_block, 0)

    for copy in zs:
        copy.wait()
    own_z = pl.multiple_of(z * 256, 16)

    def add_four(n, _):
        s, j = n // 2, n % 2
        at = pl.multiple_of(j * 128, 16)
        total = buf_a[s, pl.ds(own_z + at, 128), :].astype(jnp.float32)
        for d in range(3):
            total += buf_b[d, s, pl.ds(at, 128), :].astype(jnp.float32)
        piece[s, pl.ds(at, 128), :] = total.astype(jnp.bfloat16)
        return 0

    lax.fori_loop(0, BANDS * 2, add_four, 0)
    x_mine = pl.multiple_of(xl * OWN, 16)
    x_other = pl.multiple_of((1 - xl) * OWN, 16)
    step_c = remote(piece.at[:, pl.ds(x_other, OWN)], buf_c, sc, rc, (x_peer, space))
    step_c.start()
    step_c.wait()

    def add_two(s, _):
        total = buf_c[s].astype(jnp.float32) + piece[s, pl.ds(x_mine, OWN), :].astype(
            jnp.float32
        )
        buf_c[s] = (total * (1.0 / 16.0)).astype(jnp.bfloat16)
        return 0

    lax.fori_loop(0, BANDS, add_two, 0)
    own_row = pl.multiple_of(core * half + z * 256 + xl * OWN, 16)
    ds = []
    for d in range(1, BANDS):
        ds.append(
            remote(
                buf_c.at[(space + d) % BANDS], mean.at[d, pl.ds(own_row, OWN)],
                sd.at[d - 1], rd.at[d - 1], (member, (space + d) % BANDS),
            )
        )
        ds[-1].start()
    mean[0, pl.ds(own_row, OWN), :] = buf_c[space]
    for copy in ds:
        copy.wait()
    step_e = remote(
        mean.at[:, pl.ds(own_row, OWN)], mean.at[:, pl.ds(own_row, OWN)], se, re,
        (x_peer, space),
    )
    step_e.start()
    step_e.wait()
    z_row = pl.multiple_of(core * half + z * 256, 16)
    fs = []
    for d in (1, 2, 3):
        fs.append(
            remote(
                mean.at[:, pl.ds(z_row, 256)], mean.at[:, pl.ds(z_row, 256)],
                sf.at[d - 1], rf.at[d - 1], (z_peers[d - 1], space),
            )
        )
        fs[-1].start()
    for copy in fs:
        copy.wait()
    step_g = remote(
        mean.at[:, pl.ds(mine, half)], mean.at[:, pl.ds(mine, half)], sg, rg, (c_peer, space)
    )
    step_g.start()
    step_g.wait()
    for copy in raws:
        copy.wait()

    def centre(n, _):
        s, j = n // 9, n % 9
        at = pl.multiple_of(j * 224, 16)
        d = (space + BANDS - s) % BANDS
        block = got[d, pl.ds(at, 224), :].astype(jnp.float32)
        block = block - mean[d, pl.ds(at, 224), :].astype(jnp.float32)
        out_ref[s, pl.ds(at, 224), :] = block.astype(jnp.bfloat16)
        return 0

    def own(j, _):
        at = pl.multiple_of(j * 224, 16)
        got[0, pl.ds(at, 224), :] = f_ref[space, pl.ds(at, 224), :]
        return 0

    lax.fori_loop(0, 9, own, 0)
    lax.fori_loop(0, BANDS * 9, centre, 0)


def exchange(fourier):
    block = (BANDS, ROWSP, 128)
    sem = pltpu.SemaphoreType.DMA
    bf = jnp.bfloat16
    return pl.pallas_call(
        exchange_kernel,
        name="exchange",
        out_shape=[
            jax.ShapeDtypeStruct((BANDS, ROWS, 128), bf),
            jax.ShapeDtypeStruct((BANDS * CHUNKS * GROUP, LON), bf),
        ],
        in_specs=[pl.BlockSpec(memory_space=pltpu.VMEM)],
        out_specs=[pl.BlockSpec(memory_space=pltpu.VMEM)] * 2,
        scratch_shapes=[
            pltpu.VMEM(block, bf),
            pltpu.VMEM(block, bf),
            pltpu.VMEM((BANDS, 8 * OWN, 128), bf),
            pltpu.VMEM((3, BANDS, 256, 128), bf),
            pltpu.VMEM((BANDS, OWN, 128), bf),
            pltpu.VMEM((BANDS, 256, 128), bf),
            sem((7,)), sem((7,)),
            sem, sem,
            sem((3,)), sem((3,)),
            sem, sem,
            sem((7,)), sem((7,)),
            sem, sem,
            sem((3,)), sem((3,)),
            sem, sem,
        ],
        compiler_params=pltpu.CompilerParams(
            collective_id=1, has_side_effects=True, vmem_limit_bytes=50 * 2**20
        ),
    )(fourier)


RB = 3


def synthesis_kernel(f_ref, basis_ref, scale_ref, weather_ref, out_ref):
    step = pl.program_id(0)
    rows = []
    for r in range(RB):
        x = f_ref[:, :, r].reshape(BANDS * CHUNKS * GROUP, 128)
        rows.append(x.T)
    lhs = jnp.concatenate(rows, axis=0)
    noise = jnp.dot(lhs, basis_ref[...], preferred_element_type=jnp.float32)
    for r in range(RB):
        for q in range(Q):
            scale = scale_ref[q * R + step * RB + r]
            at = (r * Q + q) * 32
            out_ref[0, q, r] = (
                weather_ref[0, q, r].astype(jnp.float32) + scale * noise[at : at + 32]
            ).astype(jnp.bfloat16)


def synthesis(fourier, basis, scale, weather):
    fourier = fourier.reshape(BANDS, CHUNKS, R, GROUP, 128)
    rows = weather.shape[2]
    weather = weather.reshape(1, Q, R, rows, LON)
    block = pl.BlockSpec((1, Q, RB, rows, LON), lambda i: (0, 0, i, 0, 0))
    out = pl.pallas_call(
        synthesis_kernel,
        name="synthesis",
        grid=(R // RB,),
        out_shape=jax.ShapeDtypeStruct(weather.shape, jnp.bfloat16),
        in_specs=[
            pl.BlockSpec((BANDS, CHUNKS, RB, GROUP, 128), lambda i: (0, 0, i, 0, 0)),
            pl.BlockSpec(basis.shape, lambda i: (0, 0)),
            pl.BlockSpec(memory_space=pltpu.SMEM),
            block,
        ],
        out_specs=block,
        compiler_params=pltpu.CompilerParams(
            dimension_semantics=("arbitrary",), vmem_limit_bytes=50 * 2**20
        ),
    )(fourier, basis, scale, weather)
    return out.reshape(1, CH, rows, LON)


def tables():
    order = lax.axis_index("space") * ORDERS + jnp.arange(CHUNKS)[:, None] * ORDP
    order = order + jnp.arange(ORDP)[None, :]
    logs = diagonal_log(BANDS * ORDERS + 2)[order]
    row_first = (LON // 2 + 1 - TCOUNT) // 2
    colatitude = (
        math.pi
        * (row_first + jnp.arange(TCOUNT, dtype=jnp.int32)).astype(jnp.float32)
        / (LON // 2)
    )
    diag = jnp.exp(
        logs[:, :, None]
        - 0.5 * math.log(4.0 * math.pi)
        + order.astype(jnp.float32)[:, :, None] * jnp.log(jnp.sin(colatitude))
    )
    return jnp.cos(colatitude)[None, :], diag


def local(weather, coefficients, channel_scale):
    cosine, diag = tables()
    fourier = transform(coefficients.transpose(0, 1, 3, 2, 4), cosine, diag)
    centred, basis = exchange(fourier)
    return synthesis(centred, basis, channel_scale, weather)


def solution(mesh):
    return jax.shard_map(
        local,
        mesh=mesh,
        in_specs=(P("member", None, "space", None), P("member", None, None, "space", None), P()),
        out_specs=P("member", None, "space", None),
        check_vma=False,
    )
```

time: 530 us -> 183 us (0.35); the launches traced: 521 us -> 182 us
  local copies, waits for them, and re-layouts: 195 us -> 1.17 us
  Pallas kernels: 0 us -> 179 us
  other arithmetic: 115 us -> 2.06 us
  blocking collectives: 98.2 us -> 0 us
  waiting for transfers between devices: 45.8 us -> 0 us
  loops' own time: 27.1 us -> 0 us
  starting transfers between devices: 21.1 us -> 0 us
  matrix products: 18.1 us -> 0 us
    pallas_call x0 -> x3, Pallas kernels: none -> 179 us  [the longest x1 120 us: exchange(): pl.pallas_call(exchange_kernel, name='exchange', out_shape=[jax.ShapeDtyp...]
    all_to_all x1 -> x0, blocking collectives: 98.2 us -> none  [local(): lax.all_to_all(perturbed, 'member', split_axis=0, concat_axis=2, tiled=True)]
    reshape x6 -> x1, local copies, waits for them, and re-layouts: 90.9 us -> 0.01 us  [the longest x1 27.3 us: exchange_both(): parts = parts.reshape(-1, *inside)]
    while x345 -> x0, other arithmetic: 53.9 us -> none
    all_to_all x2 -> x0, waiting for transfers between devices: 45.8 us -> none  [the longest x1 45.8 us: exchange_both(): parts = lax.all_to_all(parts, axis, split_axis=0, concat_axis=0, tiled=True)]
    another operation x4 -> x1, local copies, waits for them, and re-layouts: 32.1 us -> 0.12 us  [the longest x1 16.2 us: local(): banded.reshape(member_count * channels * lat_local, 2 * order_count)]
    another operation x1 -> x0, loops' own time: 27.1 us -> none  [legendre_table(): lax.scan(advance, (empty, empty), jnp.arange(turn_count, dtype=jnp.int32))]
    another operation x29 -> x3, other arithmetic: 24.8 us -> 0.42 us
  transfers between devices with their start and end apart: 2 -> 0, of which waited for: 1 -> 0; matrix products, arithmetic and copies ran while one was open for 24% -> 0% of each run, Pallas kernels for 0% -> 0%
where the time goes in v1:
time: 183 us; the launch traced here: 182 us
  Pallas kernels  179 us (98%)
  other arithmetic  2.06 us (1%)
    pallas_call x1, Pallas kernels, exchange(): pl.pallas_call(exchange_kernel, name='exchange', out_shape=[jax.ShapeDtyp...  120 us
    pallas_call x1, Pallas kernels, transform(): pl.pallas_call(transform_kernel, name='transform', out_shape=jax.ShapeDty...  45.8 us
    pallas_call x1, Pallas kernels, synthesis(): pl.pallas_call(synthesis_kernel, name='synthesis', grid=(R // RB,), out_s...  12.7 us

profile of v1, /device:TPU:1, one launch (start us, length us, event | category | flops | bytes accessed | tf_op | source)
XLA Modules:
  0.0 182.2 jit_solution(8030076663512973641)
XLA Ops:
  0.0 0.1 add_convert_fusion
  0.1 0.1 compare_select_fusion
  0.2 0.1 reshape.123
  0.2 0.6 multiply_cosine_fusion.cos_ref
  0.9 0.3 reduce-window.9
  1.2 0.1 slice.10
  1.4 0.1 slice_reduce_fusion
  1.5 0.1 add_bitcast_fusion
  1.6 0.1 pad_maximum_fusion
  1.6 0.8 gather_fusion
  2.4 0.1 reshape.131
  2.5 0.7 add_exponential_fusion.diag_ref
  3.2 0.0 copy-start
  3.2 45.8 %transform.1.f_ref = bf16[8,2048,128]{2,1,0:T(8,128)(2,1)} custom-call(s32[1,84,46,2,361]{4,3,2,1,0:T(2,128)} %bitcast.11, f32[1,256]{1,0:T(1,128)} %multiply_cosine_fusion.cos_ref, f32[2,24,256]{2,1,0:T(8,128)} %add_exponential_fusion.diag_ref), custom_call_target="tpu_custom_call" | custom-call | tf_op jit(solution)/shard_map/transform/pallas_call | solution.py:203
  49.1 120.4 %exchange.1 = (bf16[8,2016,128]{2,1,0:T(8,128)(2,1)}, bf16[768,1440]{1,0:T(8,128)(2,1)S(1)}) custom-call(bf16[8,2048,128]{2,1,0:T(8,128)(2,1)} %transform.1.f_ref), custom_call_target="tpu_custom_call" | custom-call | tf_op jit(solution)/shard_map/exchange/pallas_call | solution.py:396
  169.5 0.0 copy-done
  169.5 12.7 %synthesis.1 = bf16[1,4,21,32,1440]{4,3,2,1,0:T(8,128)(2,1)} custom-call(bf16[8,2,21,48,128]{4,3,2,1,0:T(8,128)(2,1)} %bitcast.13, bf16[768,1440]{1,0:T(8,128)(2,1)S(1)} %get-tuple-element.8.basis_ref, f32[84]{0:T(128)S(1)} %copy-done, bf16[1,4,21,32,1440]{4,3,2,1,0:T(8,128)(2,1)} %bitcast.12), custom_call_target="tpu_custom_call" | custom-call | tf_op jit(solution)/shard_map/synthesis/pallas_call | solution.py:452
  (7 shorter events, 0.1 us)
Async XLA Ops:
  3.2 166.2 %copy-start = (f32[84]{0:T(128)S(1)}, f32[84]{0:T(128)}, u32[]{:S(2)}) copy-start(f32[84]{0:T(128)} %scale_ref.1) | copy-start | bytes 1012

commit v2 on v1

v2 whole, which is shorter than its diff:
```python
import functools
import math

import jax
import jax.numpy as jnp
from jax import lax
from jax.experimental import pallas as pl
from jax.experimental.pallas import tpu as pltpu
from jax.sharding import PartitionSpec as P

MESH = pl.DeviceIdType.MESH

CH = 84
LON = 1440
TCOUNT = 256
LP = 361
BANDS = 8
ORDERS = 46
CHUNKS = 2
ORDP = 24
Q = 4
R = CH // Q
RP = 24
MROWS = 2 * Q * RP
MP = MROWS + 8
LROWS = 392
GROUP = 2 * ORDP
PIECE = R * GROUP
PIECEP = 1024
OWN = 128
FACTOR = math.sqrt(3.0) * math.sqrt(4.0 * math.pi) / LP * 2.0 ** (-30)


def diagonal_log(order_count):
    steps_up = jnp.arange(1, order_count, dtype=jnp.int32).astype(jnp.float32)
    terms = 0.5 * jnp.log((2.0 * steps_up + 1.0) / (2.0 * steps_up))
    return jnp.concatenate([jnp.zeros((1,), jnp.float32), jnp.cumsum(terms)])


def lane_blocks(values, lane):
    low = lane < 64

    def swap(a, b, width, mask):
        ra = pltpu.roll(a, 128 - width, 1)
        rb = pltpu.roll(b, width, 1)
        return jnp.where(mask, a, rb), jnp.where(mask, ra, b)

    v0, v1, v2, v3 = values
    a0, a2 = swap(v0, v2, 64, low)
    a1, a3 = swap(v1, v3, 64, low)
    even = (lane % 64) < 32
    b0, b1 = swap(a0, a1, 32, even)
    b2, b3 = swap(a2, a3, 32, even)
    return b0, b1, b2, b3


def fourier_kernel(
    coef_ref, cos_ref, diag_ref, out_ref, basis_ref,
    coef_v, lhs_v, tab, stage, f, got, mean, buf_a, buf_b, buf_c, piece,
    sems, raw_s, raw_r, sa, ra, sb, rb, sc, rc, sd, rd, sf, rf, sg, rg,
):
    member, space = lax.axis_index("member"), lax.axis_index("space")
    z, xl, core = member // 4, (member // 2) % 2, member % 2

    def member_of(z, xl, core):
        return (z * 2 + xl) * 2 + core

    cuts = (0, 32, 64, CH)
    loads = [
        pltpu.make_async_copy(
            coef_ref.at[0, pl.ds(lo, hi - lo)], coef_v.at[pl.ds(lo, hi - lo)], sems.at[n]
        )
        for n, (lo, hi) in enumerate(zip(cuts[:-1], cuts[1:]))
    ]
    for load in loads:
        load.start()

    z_peers = [member_of((z + d) % 4, xl, core) for d in (1, 2, 3)]
    x_peer = member_of(z, 1 - xl, core)
    c_peer = member_of(z, xl, 1 - core)
    s_peers = [(space + d) % BANDS for d in range(1, BANDS)]
    barrier = pltpu.get_barrier_semaphore()
    for peer in z_peers + [x_peer, c_peer]:
        pl.semaphore_signal(barrier, inc=1, device_id=(peer, space), device_id_type=MESH)
    for peer in s_peers:
        pl.semaphore_signal(barrier, inc=1, device_id=(member, peer), device_id_type=MESH)

    def clear_lhs(n, _):
        lhs_v[2, pl.ds(pl.multiple_of(n * MP, 8), MP), :] = jnp.zeros((MP, 128), jnp.float32)
        for h in range(2):
            for at in range(LP // 8 * 8, 384, 8):
                tab[h, pl.ds(pl.multiple_of(n * LROWS + at, 8), 8), :] = jnp.zeros(
                    (8, 128), jnp.float32
                )
        return 0

    lax.fori_loop(0, ORDP, clear_lhs, 0)
    for k in range(CHUNKS):
        for s in range(BANDS):
            f[k, s, pl.ds(PIECE, PIECEP - PIECE), :] = jnp.zeros(
                (PIECEP - PIECE, 128), jnp.bfloat16
            )

    def arrange(k, c):
        base = c // R * 48 + c % R
        for i in range(min(ORDP, ORDERS - k * ORDP)):
            for t in range(3):
                wide = min(128, LP - 128 * t)
                raw = coef_v[c, k * ORDP + i, :, pl.ds(128 * t, wide)]
                lhs_v[t, pl.ds(i * MP + base, 2, stride=RP), pl.ds(0, wide)] = (
                    raw.astype(jnp.float32) * FACTOR
                )

    def table(k, ready):
        first = space * ORDERS + k * ORDP
        order = (first + lax.broadcasted_iota(jnp.int32, (ORDP, 128), 0)).astype(jnp.float32)
        square = order * order
        order_wide = first + lax.broadcasted_iota(jnp.int32, (ORDP, TCOUNT), 0)
        cosine = jnp.broadcast_to(cos_ref[...], (ORDP, TCOUNT))
        diag = diag_ref[k]
        older = jnp.zeros((ORDP, TCOUNT), jnp.float32)
        newer = jnp.zeros((ORDP, TCOUNT), jnp.float32)
        for tile in range(3):
            degree = tile * 128 + lax.broadcasted_iota(jnp.int32, (ORDP, 128), 1)
            degree = degree.astype(jnp.float32)
            degree_square = degree * degree
            prior = degree - 1.0
            up = jnp.sqrt(
                jnp.maximum(4.0 * degree_square - 1.0, 1.0)
                / jnp.maximum(degree_square - square, 1.0)
            )
            down = jnp.sqrt(
                jnp.maximum(prior * prior - square, 0.0)
                / jnp.maximum(4.0 * prior * prior - 1.0, 1.0)
            )

            def block(j, carry, steps=8, channels=True):
                older, newer, up, down = carry
                for u in range(steps):
                    deg = tile * 128 + j * 8 + u
                    nxt = up[:, u : u + 1] * (cosine * newer - down[:, u : u + 1] * older)
                    nxt = jnp.where(order_wide == deg, diag, nxt)
                    for b in range(ORDP // 8):
                        for h in range(2):
                            tab[h, pl.ds(b * 8 * LROWS + deg, 8, stride=LROWS), :] = nxt[
                                8 * b : 8 * b + 8, 128 * h : 128 * h + 128
                            ]
                    older, newer = newer, nxt
                if channels:
                    for n in range(2):
                        arrange(k, tile * 32 + j * 2 + n)
                return older, newer, pltpu.roll(up, 120, 1), pltpu.roll(down, 120, 1)

            if not ready:
                loads[tile].wait()
            whole = (cuts[tile + 1] - cuts[tile]) // 2
            carry = lax.fori_loop(0, whole, block, (older, newer, up, down))
            if tile == 2:
                count = (LP - 128 * tile) // 8
                carry = lax.fori_loop(
                    whole, count, functools.partial(block, channels=False), carry
                )
                block(count, carry, steps=LP % 8, channels=False)
            older, newer = carry[:2]

    lane = lax.broadcasted_iota(jnp.int32, (RP * 2, 128), 1)

    def orders_of(k):
        def one(n, _):
            for i in (2 * n, 2 * n + 1):
                row = pl.multiple_of(i * MP, 8)
                lhs = jnp.concatenate(
                    [lhs_v[t, pl.ds(row, MROWS), :].astype(jnp.bfloat16) for t in range(3)],
                    axis=1,
                )
                row = pl.multiple_of(i * LROWS, 8)
                rhs = jnp.concatenate(
                    [tab[h, pl.ds(row, 384), :].astype(jnp.bfloat16) for h in range(2)], axis=1
                )
                out = jnp.dot(lhs, rhs, preferred_element_type=jnp.float32)
                for h in range(2):
                    parts = [
                        out[48 * q : 48 * q + 48, 128 * h : 128 * h + 128] for q in range(Q)
                    ]
                    for b, part in enumerate(lane_blocks(parts, lane)):
                        s = 4 * h + b
                        for a in range(6):
                            stage[
                                pl.ds((s * 48 + 8 * a) * ORDP + i, 8, stride=ORDP), :
                            ] = part[8 * a : 8 * a + 8]
            return 0

        lax.fori_loop(0, min(ORDP, ORDERS - k * ORDP) // 2, one, 0)

        def pack(n, _):
            s = n // 7
            for u in range(3):
                r = n % 7 * 3 + u
                first = stage[pl.ds(pl.multiple_of((s * 48 + r) * ORDP, 8), ORDP), :]
                second = stage[pl.ds(pl.multiple_of((s * 48 + RP + r) * ORDP, 8), ORDP), :]
                both = jnp.concatenate([first, second], axis=0).astype(jnp.bfloat16)
                f[k, s, pl.ds(pl.multiple_of(r * GROUP, 16), GROUP), :] = both
            return 0

        lax.fori_loop(0, BANDS * 7, pack, 0)

    def clear_stage(n, _):
        for i in range(ORDERS - ORDP, ORDP):
            stage[pl.ds(n * 8 * ORDP + i, 8, stride=ORDP), :] = jnp.zeros(
                (8, 128), jnp.float32
            )
        return 0

    def remote(src, dst, ss, rs, device):
        return pltpu.make_async_remote_copy(
            src_ref=src, dst_ref=dst, send_sem=ss, recv_sem=rs,
            device_id=device, device_id_type=MESH,
        )

    half = PIECEP // 2
    mine = pl.multiple_of(core * half, 16)
    other = pl.multiple_of((1 - core) * half, 16)
    in_half = pl.multiple_of(z * OWN, 16)
    own_row = pl.multiple_of(core * half + z * OWN, 16)

    def pair_sum(k):
        return remote(
            f.at[k, :, pl.ds(other, half)], buf_a.at[k], sa.at[k], ra.at[k], (c_peer, space)
        )

    def z_sums(k):
        return [
            remote(
                buf_a.at[k, :, pl.ds(pl.multiple_of((z + d) % 4 * OWN, 16), OWN)],
                buf_b.at[k, d - 1],
                sb.at[k, d - 1], rb.at[k, d - 1], (z_peers[d - 1], space),
            )
            for d in (1, 2, 3)
        ]

    def x_sum(k):
        return remote(piece.at[k], buf_c.at[k], sc.at[k], rc.at[k], (x_peer, space))

    def means_out(k):
        return [
            remote(
                buf_c.at[k, (space + d) % BANDS], mean.at[k, d, pl.ds(own_row, OWN)],
                sd.at[k, d - 1], rd.at[k, d - 1], (member, (space + d) % BANDS),
            )
            for d in range(1, BANDS)
        ]

    def z_gather(k):
        return [
            remote(
                mean.at[k, :, pl.ds(own_row, OWN)], mean.at[k, :, pl.ds(own_row, OWN)],
                sf.at[k, d - 1], rf.at[k, d - 1], (z_peers[d - 1], space),
            )
            for d in (1, 2, 3)
        ]

    def core_gather(k):
        return remote(
            mean.at[k, :, pl.ds(mine, half)], mean.at[k, :, pl.ds(mine, half)],
            sg.at[k], rg.at[k], (c_peer, space),
        )

    def raw(k, part, at, size):
        return [
            remote(
                f.at[k, (space + d) % BANDS, pl.ds(at, size)], got.at[k, d, pl.ds(at, size)],
                raw_s.at[part, d - 1], raw_r.at[part, d - 1],
                (member, (space + d) % BANDS),
            )
            for d in range(1, BANDS)
        ]

    def begin(copies):
        for copy in copies:
            copy.start()

    def finish(copies):
        for copy in copies:
            copy.wait()

    def add_pair(k):
        def one(n, _):
            s, at = n // 4, pl.multiple_of(n % 4 * OWN, 16)
            total = buf_a[k, s, pl.ds(at, OWN), :].astype(jnp.float32)
            total += f[k, s, pl.ds(mine + at, OWN), :].astype(jnp.float32)
            buf_a[k, s, pl.ds(at, OWN), :] = total.astype(jnp.bfloat16)
            return 0

        lax.fori_loop(0, BANDS * 4, one, 0)

    def add_four(k):
        def one(s, _):
            total = buf_a[k, s, pl.ds(in_half, OWN), :].astype(jnp.float32)
            for d in range(3):
                total += buf_b[k, d, s].astype(jnp.float32)
            piece[k, s] = total.astype(jnp.bfloat16)
            return 0

        lax.fori_loop(0, BANDS, one, 0)

    def add_two(k):
        def one(s, _):
            total = buf_c[k, s].astype(jnp.float32) + piece[k, s].astype(jnp.float32)
            buf_c[k, s] = (total * (1.0 / 16.0)).astype(jnp.bfloat16)
            return 0

        lax.fori_loop(0, BANDS, one, 0)
        mean[k, 0, pl.ds(own_row, OWN), :] = buf_c[k, space]

    def centre(k):
        def one(n, _):
            d, at = n // 9, pl.multiple_of(n % 9 * 112, 16)
            s = (space + BANDS - d) % BANDS
            block = got[k, d, pl.ds(at, 112), :].astype(jnp.float32)
            block = block - mean[k, d, pl.ds(at, 112), :].astype(jnp.float32)
            out_ref[s, k, pl.ds(at, 112), :] = block.astype(jnp.bfloat16)
            return 0

        def own(n, _):
            at = pl.multiple_of(n * 112, 16)
            block = f[k, space, pl.ds(at, 112), :].astype(jnp.float32)
            block = block - mean[k, 0, pl.ds(at, 112), :].astype(jnp.float32)
            out_ref[space, k, pl.ds(at, 112), :] = block.astype(jnp.bfloat16)
            return 0

        lax.fori_loop(9, BANDS * 9, one, 0)
        lax.fori_loop(0, 9, own, 0)

    column = lax.broadcasted_iota(jnp.int32, (ORDP, LON), 1).astype(jnp.float32)
    index = lax.broadcasted_iota(jnp.int32, (ORDP, LON), 0)

    def basis():
        def one(n, _):
            order = n // CHUNKS * ORDERS + n % CHUNKS * ORDP + index
            product = order.astype(jnp.float32) * column
            turns = jnp.floor((product + 0.5) * (1.0 / LON))
            angle = 2.0 * math.pi / LON * (product - turns * LON)
            weight = jnp.where(order == 0, 1.0, math.sqrt(2.0))
            weight = jnp.where(n % CHUNKS * ORDP + index < ORDERS, weight, 0.0)
            both = jnp.concatenate(
                [weight * jnp.cos(angle), weight * jnp.sin(angle)], axis=0
            )
            basis_ref[pl.ds(pl.multiple_of(n * GROUP, 16), GROUP), :] = both.astype(
                jnp.bfloat16
            )
            return 0

        lax.fori_loop(0, BANDS * CHUNKS, one, 0)

    table(0, False)
    orders_of(0)
    pl.semaphore_wait(barrier, 5 + BANDS - 1)
    a0, a1 = pair_sum(0), pair_sum(1)
    a0.start()
    raw0 = raw(0, 0, 0, PIECE)
    begin(raw0)
    lax.fori_loop(0, BANDS * 48 // 8, clear_stage, 0)
    table(1, True)
    a0.wait()
    add_pair(0)
    b0, b1 = z_sums(0), z_sums(1)
    begin(b0)
    orders_of(1)
    a1.start()
    finish(b0)
    add_four(0)
    c0, c1 = x_sum(0), x_sum(1)
    c0.start()
    a1.wait()
    add_pair(1)
    begin(b1)
    basis()
    c0.wait()
    add_two(0)
    d0, d1 = means_out(0), means_out(1)
    begin(d0)
    finish(b1)
    add_four(1)
    c1.start()
    raw1 = raw(1, 1, 0, 512)
    begin(raw1)
    finish(d0)
    f0, f1 = z_gather(0), z_gather(1)
    begin(f0)
    c1.wait()
    add_two(1)
    begin(d1)
    raw2 = raw(1, 2, 512, PIECE - 512)
    begin(raw2)
    finish(f0)
    g0, g1 = core_gather(0), core_gather(1)
    g0.start()
    finish(d1)
    begin(f1)
    finish(raw0)
    g0.wait()
    centre(0)
    finish(f1)
    g1.start()
    finish(raw1)
    finish(raw2)
    g1.wait()
    centre(1)


def fourier_blocks(coefficients, cosine, diag):
    sem = pltpu.SemaphoreType.DMA
    bf = jnp.bfloat16
    return pl.pallas_call(
        fourier_kernel,
        name="fourier_blocks",
        out_shape=[
            jax.ShapeDtypeStruct((BANDS, CHUNKS, PIECE, 128), bf),
            jax.ShapeDtypeStruct((BANDS * CHUNKS * GROUP, LON), bf),
        ],
        in_specs=[
            pl.BlockSpec(memory_space=pl.ANY),
            pl.BlockSpec(memory_space=pltpu.VMEM),
            pl.BlockSpec(memory_space=pltpu.VMEM),
        ],
        out_specs=[pl.BlockSpec(memory_space=pltpu.VMEM)] * 2,
        scratch_shapes=[
            pltpu.VMEM((CH, ORDERS, 2, LP), jnp.int32),
            pltpu.VMEM((3, ORDP * MP, 128), jnp.float32),
            pltpu.VMEM((2, ORDP * LROWS, 128), jnp.float32),
            pltpu.VMEM((BANDS * 48 * ORDP, 128), jnp.float32),
            pltpu.VMEM((CHUNKS, BANDS, PIECEP, 128), bf),
            pltpu.VMEM((CHUNKS, BANDS, PIECE, 128), bf),
            pltpu.VMEM((CHUNKS, BANDS, PIECEP, 128), bf),
            pltpu.VMEM((CHUNKS, BANDS, PIECEP // 2, 128), bf),
            pltpu.VMEM((CHUNKS, 3, BANDS, OWN, 128), bf),
            pltpu.VMEM((CHUNKS, BANDS, OWN, 128), bf),
            pltpu.VMEM((CHUNKS, BANDS, OWN, 128), bf),
            sem((3,)),
            sem((3, 7)), sem((3, 7)),
            sem((2,)), sem((2,)),
            sem((2, 3)), sem((2, 3)),
            sem((2,)), sem((2,)),
            sem((2, 7)), sem((2, 7)),
            sem((2, 3)), sem((2, 3)),
            sem((2,)), sem((2,)),
        ],
        compiler_params=pltpu.CompilerParams(
            collective_id=1, has_side_effects=True, vmem_limit_bytes=63 * 2**20
        ),
    )(coefficients, cosine, diag)


RB = 3


def synthesis_kernel(f_ref, basis_ref, scale_ref, weather_ref, out_ref):
    step = pl.program_id(0)
    rows = []
    for r in range(RB):
        x = f_ref[:, :, r].reshape(BANDS * CHUNKS * GROUP, 128)
        rows.append(x.T)
    lhs = jnp.concatenate(rows, axis=0)
    noise = jnp.dot(lhs, basis_ref[...], preferred_element_type=jnp.float32)
    for r in range(RB):
        for q in range(Q):
            scale = scale_ref[q * R + step * RB + r]
            at = (r * Q + q) * 32
            out_ref[0, q, r] = (
                weather_ref[0, q, r].astype(jnp.float32) + scale * noise[at : at + 32]
            ).astype(jnp.bfloat16)


def synthesis(fourier, basis, scale, weather):
    fourier = fourier.reshape(BANDS, CHUNKS, R, GROUP, 128)
    rows = weather.shape[2]
    weather = weather.reshape(1, Q, R, rows, LON)
    block = pl.BlockSpec((1, Q, RB, rows, LON), lambda i: (0, 0, i, 0, 0))
    out = pl.pallas_call(
        synthesis_kernel,
        name="synthesis",
        grid=(R // RB,),
        out_shape=jax.ShapeDtypeStruct(weather.shape, jnp.bfloat16),
        in_specs=[
            pl.BlockSpec((BANDS, CHUNKS, RB, GROUP, 128), lambda i: (0, 0, i, 0, 0)),
            pl.BlockSpec(basis.shape, lambda i: (0, 0)),
            pl.BlockSpec(memory_space=pltpu.SMEM),
            block,
        ],
        out_specs=block,
        compiler_params=pltpu.CompilerParams(
            dimension_semantics=("arbitrary",), vmem_limit_bytes=50 * 2**20
        ),
    )(fourier, basis, scale, weather)
    return out.reshape(1, CH, rows, LON)


def tables():
    order = lax.axis_index("space") * ORDERS + jnp.arange(CHUNKS)[:, None] * ORDP
    order = order + jnp.arange(ORDP)[None, :]
    logs = diagonal_log(BANDS * ORDERS + 2)[order]
    row_first = (LON // 2 + 1 - TCOUNT) // 2
    colatitude = (
        math.pi
        * (row_first + jnp.arange(TCOUNT, dtype=jnp.int32)).astype(jnp.float32)
        / (LON // 2)
    )
    diag = jnp.exp(
        logs[:, :, None]
        - 0.5 * math.log(4.0 * math.pi)
        + order.astype(jnp.float32)[:, :, None] * jnp.log(jnp.sin(colatitude))
    )
    return jnp.cos(colatitude)[None, :], diag


def local(weather, coefficients, channel_scale):
    cosine, diag = tables()
    centred, basis = fourier_blocks(coefficients.transpose(0, 1, 3, 2, 4), cosine, diag)
    return synthesis(centred, basis, channel_scale, weather)


def solution(mesh):
    return jax.shard_map(
        local,
        mesh=mesh,
        in_specs=(P("member", None, "space", None), P("member", None, None, "space", None), P()),
        out_specs=P("member", None, "space", None),
        check_vma=False,
    )
```

time: 183 us -> 121 us (0.66)
  Pallas kernels: 179 us -> 116 us
    pallas_call x2 -> x1, Pallas kernels: 166 us -> 103 us  [fourier_blocks(): pl.pallas_call(fourier_kernel, name='fourier_blocks', out_shape=[jax.Shap...]
where the time goes in v2:
time: 121 us
  Pallas kernels  116 us (96%)
  local copies, waits for them, and re-layouts  2.83 us (2%)
  other arithmetic  2.06 us (2%)
    pallas_call x1, Pallas kernels, fourier_blocks(): pl.pallas_call(fourier_kernel, name='fourier_blocks', out_shape=[jax.Shap...  103 us
    pallas_call x1, Pallas kernels, synthesis(): pl.pallas_call(synthesis_kernel, name='synthesis', grid=(R // RB,), out_s...  12.7 us

profile of v2, /device:TPU:1, one launch (start us, length us, event | category | flops | bytes accessed | tf_op | source)
XLA Modules:
  0.0 120.9 jit_solution(10930971693169440081)
XLA Ops:
  0.0 0.0 copy-start.1
  0.0 0.1 add_convert_fusion
  0.1 0.1 compare_select_fusion
  0.2 0.1 reshape.123
  0.2 0.6 multiply_cosine_fusion.cos_ref
  0.9 0.3 reduce-window.9
  1.3 0.1 slice.10
  1.4 0.1 slice_reduce_fusion
  1.5 0.1 add_bitcast_fusion
  1.6 0.1 pad_maximum_fusion
  1.6 0.8 gather_fusion
  2.5 0.1 reshape.131
  2.5 0.7 add_exponential_fusion.diag_ref
  3.3 103.3 %fourier_blocks.1 = (bf16[8,2,1008,128]{3,2,1,0:T(8,128)(2,1)}, bf16[768,1440]{1,0:T(8,128)(2,1)}) custom-call(s32[1,84,46,2,361]{4,3,2,1,0:T(2,128)} %bitcast.11, f32[1,256]{1,0:T(1,128)} %multiply_cosine_fusion.cos_ref, f32[2,24,256]{2,1,0:T(8,128)} %add_exponential_fusion.diag_ref), custom_call_target="tpu_custom_call" | custom-call | tf_op jit(solution)/shard_map/fourier_blocks/pallas_call | solution.py:414
  106.5 0.0 copy-done.1
  106.5 0.0 copy-start
  106.5 1.7 %copy-done = bf16[768,1440]{1,0:T(8,128)(2,1)S(1)} copy-done((bf16[768,1440]{1,0:T(8,128)(2,1)S(1)}, bf16[768,1440]{1,0:T(8,128)(2,1)}, u32[]{:S(2)}) %copy-start) | copy-done | bytes 2211864
  108.2 12.7 %synthesis.1 = bf16[1,4,21,32,1440]{4,3,2,1,0:T(8,128)(2,1)} custom-call(bf16[8,2,21,48,128]{4,3,2,1,0:T(8,128)(2,1)} %bitcast.13, bf16[768,1440]{1,0:T(8,128)(2,1)S(1)} %copy-done, f32[84]{0:T(128)S(1)} %copy-done.1, bf16[1,4,21,32,1440]{4,3,2,1,0:T(8,128)(2,1)} %bitcast.12), custom_call_target="tpu_custom_call" | custom-call | tf_op jit(solution)/shard_map/synthesis/pallas_call | solution.py:479
  (7 shorter events, 0.1 us)
Async XLA Ops:
  0.0 106.5 %copy-start.1 = (f32[84]{0:T(128)S(1)}, f32[84]{0:T(128)}, u32[]{:S(2)}) copy-start(f32[84]{0:T(128)} %scale_ref.1) | copy-start | bytes 1012
  106.5 1.7 %copy-start = (bf16[768,1440]{1,0:T(8,128)(2,1)S(1)}, bf16[768,1440]{1,0:T(8,128)(2,1)}, u32[]{:S(2)}) copy-start(bf16[768,1440]{1,0:T(8,128)(2,1)} %get-tuple-element.8.basis_ref) | copy-start | bytes 6635524

commit v3 on v2

v3 whole, which is shorter than its diff:
```python
import functools
import math

import jax
import jax.numpy as jnp
from jax import lax
from jax.experimental import pallas as pl
from jax.experimental.pallas import tpu as pltpu
from jax.sharding import PartitionSpec as P

MESH = pl.DeviceIdType.MESH

CH = 84
LON = 1440
TCOUNT = 256
LP = 361
BANDS = 8
ORDERS = 46
CHUNKS = 2
GO = 8
GROUPS = 6
PER = 3
Q = 4
R = CH // Q
RP = 24
MROWS = 2 * Q * RP
LROWS = 392
GR = R * 2 * GO
PIECE = PER * GR
PIECEP = 1024
OWN = 128
FACTOR = math.sqrt(3.0) * math.sqrt(4.0 * math.pi) / LP * 2.0 ** (-30)


def lane_blocks(values, lane):
    low = lane < 64

    def swap(a, b, width, mask):
        ra = pltpu.roll(a, 128 - width, 1)
        rb = pltpu.roll(b, width, 1)
        return jnp.where(mask, a, rb), jnp.where(mask, ra, b)

    v0, v1, v2, v3 = values
    a0, a2 = swap(v0, v2, 64, low)
    a1, a3 = swap(v1, v3, 64, low)
    even = (lane % 64) < 32
    b0, b1 = swap(a0, a1, 32, even)
    b2, b3 = swap(a2, a3, 32, even)
    return b0, b1, b2, b3


def fourier_kernel(
    coef_ref, out_ref, basis_out,
    coef_v, lhs_v, tab, factors, stage, basis_v, f, got, mean, buf_a, buf_b, buf_c, piece,
    load_sem, out_sem, basis_sem,
    raw_s, raw_r, sa, ra, sb, rb, sc, rc, sd, rd, sf, rf, sg, rg,
):
    member, space = lax.axis_index("member"), lax.axis_index("space")
    z, xl, core = member // 4, (member // 2) % 2, member % 2

    def member_of(z, xl, core):
        return (z * 2 + xl) * 2 + core

    def real(g):
        return min(GO, ORDERS - g * GO)

    loads = [
        pltpu.make_async_copy(
            coef_ref.at[0, :, pl.ds(g * GO, real(g))],
            coef_v.at[:, pl.ds(g * GO, real(g))],
            load_sem.at[g],
        )
        for g in range(GROUPS)
    ]
    for load in loads:
        load.start()

    z_peers = [member_of((z + d) % 4, xl, core) for d in (1, 2, 3)]
    x_peer = member_of(z, 1 - xl, core)
    c_peer = member_of(z, xl, 1 - core)
    s_peers = [(space + d) % BANDS for d in range(1, BANDS)]
    barrier = pltpu.get_barrier_semaphore()
    for peer in z_peers + [x_peer, c_peer]:
        pl.semaphore_signal(barrier, inc=1, device_id=(peer, space), device_id_type=MESH)
    for peer in s_peers:
        pl.semaphore_signal(barrier, inc=1, device_id=(member, peer), device_id_type=MESH)

    def clear_pads(n, _):
        lhs_v[2, pl.ds(pl.multiple_of(n * MROWS, 8), MROWS), :] = jnp.zeros(
            (MROWS, 128), jnp.float32
        )
        for h in range(2):
            for at in range(LP // 8 * 8, 384, 8):
                tab[h, pl.ds(pl.multiple_of(n * LROWS + at, 8), 8), :] = jnp.zeros(
                    (8, 128), jnp.float32
                )
        return 0

    lax.fori_loop(0, GO, clear_pads, 0)
    for k in range(CHUNKS):
        for s in range(BANDS):
            f[k, s, pl.ds(PIECE, PIECEP - PIECE), :] = jnp.zeros(
                (PIECEP - PIECE, 128), jnp.bfloat16
            )

    row_first = (LON // 2 + 1 - TCOUNT) // 2
    colatitude = (
        math.pi
        * (row_first + lax.broadcasted_iota(jnp.int32, (GO, TCOUNT), 1)).astype(jnp.float32)
        / (LON // 2)
    )
    cosine = jnp.cos(colatitude)
    log_sine = jnp.log(jnp.sin(colatitude))

    def arrange(g, c, i):
        base = c // R * 48 + c % R
        for t in range(3):
            wide = min(128, LP - 128 * t)
            raw = coef_v[c, g * GO + i, :, pl.ds(128 * t, wide)]
            lhs_v[t, pl.ds(i * MROWS + base, 2, stride=RP), pl.ds(0, wide)] = (
                raw.astype(jnp.float32) * FACTOR
            )

    def table(g):
        first = space * ORDERS + g * GO
        order_wide = first + lax.broadcasted_iota(jnp.int32, (GO, TCOUNT), 0)
        order = (first + lax.broadcasted_iota(jnp.int32, (GO, 128), 0)).astype(jnp.float32)
        square = order * order
        degrees = [
            (tile * 128 + lax.broadcasted_iota(jnp.int32, (GO, 128), 1)).astype(jnp.float32)
            for tile in range(3)
        ]
        logs = jnp.zeros((GO, 1), jnp.float32)
        for degree in degrees:
            at_least = jnp.maximum(degree, 1.0)
            term = 0.5 * jnp.log((2.0 * at_least + 1.0) / (2.0 * at_least))
            term = jnp.where((degree >= 1.0) & (degree <= order), term, 0.0)
            logs += jnp.sum(term, axis=1, keepdims=True)
        diag = jnp.exp(
            logs - 0.5 * math.log(4.0 * math.pi) + order_wide.astype(jnp.float32) * log_sine
        )

        def spread(tile, _):
            degree = tile * 128 + lax.broadcasted_iota(jnp.int32, (GO, 128), 1)
            degree = degree.astype(jnp.float32)
            degree_square = degree * degree
            prior = degree - 1.0
            up = jnp.sqrt(
                jnp.maximum(4.0 * degree_square - 1.0, 1.0)
                / jnp.maximum(degree_square - square, 1.0)
            )
            down = up * jnp.sqrt(
                jnp.maximum(prior * prior - square, 0.0)
                / jnp.maximum(4.0 * prior * prior - 1.0, 1.0)
            )
            for u in range(128):
                row = pl.multiple_of((tile * 128 + u) * GO, 8)
                factors[0, pl.ds(row, GO), :] = jnp.broadcast_to(up[:, u : u + 1], (GO, 128))
                factors[1, pl.ds(row, GO), :] = jnp.broadcast_to(down[:, u : u + 1], (GO, 128))
            return 0

        lax.fori_loop(0, 3, spread, 0)
        loads[g].wait()
        half_order = order_wide[:, :128]

        def block(j, carry, steps=8, channels=True):
            older, newer = carry
            for u in range(steps):
                deg = j * 8 + u
                row = pl.multiple_of(deg * GO, 8)
                up = factors[0, pl.ds(row, GO), :]
                down = factors[1, pl.ds(row, GO), :]
                here = half_order == deg
                fresh = []
                for h in range(2):
                    at = slice(128 * h, 128 * h + 128)
                    seed = jnp.where(here, diag[:, at], 0.0)
                    value = (up * cosine[:, at]) * newer[h] + (seed - down * older[h])
                    tab[h, pl.ds(deg, 8, stride=LROWS), :] = value
                    fresh.append(value)
                older, newer = newer, tuple(fresh)
                if channels:
                    for i in (u % 4 * 2, u % 4 * 2 + 1):
                        if i < real(g):
                            arrange(g, j * 2 + u // 4, i)
            return older, newer

        zero = jnp.zeros((GO, 128), jnp.float32)
        carry = ((zero, zero), (zero, zero))
        carry = lax.fori_loop(0, CH // 2, block, carry)
        carry = lax.fori_loop(
            CH // 2, LP // 8, functools.partial(block, channels=False), carry
        )
        block(LP // 8, carry, steps=LP % 8, channels=False)

    lane = lax.broadcasted_iota(jnp.int32, (RP * 2, 128), 1)

    def orders_of(g):
        k, at_group = g // PER, g % PER * GR

        def one(n, _):
            for i in (2 * n, 2 * n + 1):
                row = pl.multiple_of(i * MROWS, 8)
                lhs = jnp.concatenate(
                    [lhs_v[t, pl.ds(row, MROWS), :].astype(jnp.bfloat16) for t in range(3)],
                    axis=1,
                )
                row = pl.multiple_of(i * LROWS, 8)
                rhs = jnp.concatenate(
                    [tab[h, pl.ds(row, 384), :].astype(jnp.bfloat16) for h in range(2)], axis=1
                )
                out = jnp.dot(lhs, rhs, preferred_element_type=jnp.float32)
                for h in range(2):
                    parts = [
                        out[48 * q : 48 * q + 48, 128 * h : 128 * h + 128] for q in range(Q)
                    ]
                    for b, part in enumerate(lane_blocks(parts, lane)):
                        s = 4 * h + b
                        for a in range(6):
                            stage[pl.ds((s * 48 + 8 * a) * GO + i, 8, stride=GO), :] = part[
                                8 * a : 8 * a + 8
                            ]
            return 0

        if real(g) < GO:

            def clear_stage(n, _):
                for i in range(real(g), GO):
                    stage[pl.ds(n * 8 * GO + i, 8, stride=GO), :] = jnp.zeros(
                        (8, 128), jnp.float32
                    )
                return 0

            lax.fori_loop(0, BANDS * 48 // 8, clear_stage, 0)
        lax.fori_loop(0, real(g) // 2, one, 0)

        def pack(n, _):
            s = n // 3
            for u in range(7):
                r = n % 3 * 7 + u
                first = stage[pl.ds(pl.multiple_of((s * 48 + r) * GO, 8), GO), :]
                second = stage[pl.ds(pl.multiple_of((s * 48 + RP + r) * GO, 8), GO), :]
                both = jnp.concatenate([first, second], axis=0).astype(jnp.bfloat16)
                f[k, s, pl.ds(pl.multiple_of(at_group + r * 2 * GO, 16), 2 * GO), :] = both
            return 0

        lax.fori_loop(0, BANDS * 3, pack, 0)

    def remote(src, dst, ss, rs, device):
        return pltpu.make_async_remote_copy(
            src_ref=src, dst_ref=dst, send_sem=ss, recv_sem=rs,
            device_id=device, device_id_type=MESH,
        )

    half = PIECEP // 2
    mine = pl.multiple_of(core * half, 16)
    other = pl.multiple_of((1 - core) * half, 16)
    in_half = pl.multiple_of(z * OWN, 16)
    own_row = pl.multiple_of(core * half + z * OWN, 16)

    def pair_sum(k):
        return remote(
            f.at[k, :, pl.ds(other, half)], buf_a.at[k], sa.at[k], ra.at[k], (c_peer, space)
        )

    def z_sums(k):
        return [
            remote(
                buf_a.at[k, :, pl.ds(pl.multiple_of((z + d) % 4 * OWN, 16), OWN)],
                buf_b.at[k, d - 1],
                sb.at[k, d - 1], rb.at[k, d - 1], (z_peers[d - 1], space),
            )
            for d in (1, 2, 3)
        ]

    def x_sum(k):
        return remote(piece.at[k], buf_c.at[k], sc.at[k], rc.at[k], (x_peer, space))

    def means_out(k):
        return [
            remote(
                buf_c.at[k, (space + d) % BANDS], mean.at[k, d, pl.ds(own_row, OWN)],
                sd.at[k, d - 1], rd.at[k, d - 1], (member, (space + d) % BANDS),
            )
            for d in range(1, BANDS)
        ]

    def z_gather(k):
        return [
            remote(
                mean.at[k, :, pl.ds(own_row, OWN)], mean.at[k, :, pl.ds(own_row, OWN)],
                sf.at[k, d - 1], rf.at[k, d - 1], (z_peers[d - 1], space),
            )
            for d in (1, 2, 3)
        ]

    def core_gather(k):
        return remote(
            mean.at[k, :, pl.ds(mine, half)], mean.at[k, :, pl.ds(mine, half)],
            sg.at[k], rg.at[k], (c_peer, space),
        )

    def raw(k, part, at, size):
        return [
            remote(
                f.at[k, (space + d) % BANDS, pl.ds(at, size)], got.at[k, d, pl.ds(at, size)],
                raw_s.at[part, d - 1], raw_r.at[part, d - 1],
                (member, (space + d) % BANDS),
            )
            for d in range(1, BANDS)
        ]

    def begin(copies):
        for copy in copies:
            copy.start()

    def finish(copies):
        for copy in copies:
            copy.wait()

    def add_pair(k):
        def one(n, _):
            s, at = n // 4, pl.multiple_of(n % 4 * OWN, 16)
            total = buf_a[k, s, pl.ds(at, OWN), :].astype(jnp.float32)
            total += f[k, s, pl.ds(mine + at, OWN), :].astype(jnp.float32)
            buf_a[k, s, pl.ds(at, OWN), :] = total.astype(jnp.bfloat16)
            return 0

        lax.fori_loop(0, BANDS * 4, one, 0)

    def add_four(k):
        def one(s, _):
            total = buf_a[k, s, pl.ds(in_half, OWN), :].astype(jnp.float32)
            for d in range(3):
                total += buf_b[k, d, s].astype(jnp.float32)
            piece[k, s] = total.astype(jnp.bfloat16)
            return 0

        lax.fori_loop(0, BANDS, one, 0)

    def add_two(k):
        def one(s, _):
            total = buf_c[k, s].astype(jnp.float32) + piece[k, s].astype(jnp.float32)
            buf_c[k, s] = (total * (1.0 / 16.0)).astype(jnp.bfloat16)
            return 0

        lax.fori_loop(0, BANDS, one, 0)
        mean[k, 0, pl.ds(own_row, OWN), :] = buf_c[k, space]

    def outs(k, d):
        return pltpu.make_async_copy(
            got.at[k, d], out_ref.at[(space + BANDS - d) % BANDS, k], out_sem.at[k, d]
        )

    def centre(k):
        for d in range(BANDS):

            def one(n, _):
                at = pl.multiple_of(n * 112, 16)
                block = f[k, space, pl.ds(at, 112), :] if d == 0 else got[k, d, pl.ds(at, 112), :]
                block = block.astype(jnp.float32) - mean[k, d, pl.ds(at, 112), :].astype(
                    jnp.float32
                )
                got[k, d, pl.ds(at, 112), :] = block.astype(jnp.bfloat16)
                return 0

            lax.fori_loop(0, 9, one, 0)
            outs(k, d).start()

    column = lax.broadcasted_iota(jnp.int32, (GO, LON), 1).astype(jnp.float32)
    index = lax.broadcasted_iota(jnp.int32, (GO, LON), 0)

    def basis():
        def one(n, _):
            slot = n % GROUPS * GO + index
            order = n // GROUPS * ORDERS + slot
            product = order.astype(jnp.float32) * column
            turns = jnp.floor((product + 0.5) * (1.0 / LON))
            angle = 2.0 * math.pi / LON * (product - turns * LON)
            weight = jnp.where(order == 0, 1.0, math.sqrt(2.0))
            weight = jnp.where(slot < ORDERS, weight, 0.0)
            both = jnp.concatenate(
                [weight * jnp.cos(angle), weight * jnp.sin(angle)], axis=0
            )
            basis_v[pl.ds(pl.multiple_of(n * 2 * GO, 16), 2 * GO), :] = both.astype(
                jnp.bfloat16
            )
            return 0

        lax.fori_loop(0, BANDS * GROUPS, one, 0)

    def group(g):
        table(g)
        orders_of(g)

    def raw_group(part, g, at=0, size=GR):
        return raw(g // PER, part, g % PER * GR + at, size)

    a0, a1 = pair_sum(0), pair_sum(1)
    b0, b1 = z_sums(0), z_sums(1)
    c0, c1 = x_sum(0), x_sum(1)
    d0, d1 = means_out(0), means_out(1)
    f0, f1 = z_gather(0), z_gather(1)
    g0, g1 = core_gather(0), core_gather(1)
    raws = [
        raw_group(0, 0),
        raw_group(1, 1),
        raw_group(2, 2),
        raw_group(3, 3, 0, 176),
        raw_group(4, 3, 176, GR - 176),
        raw_group(5, 4),
        raw_group(6, 5),
    ]

    group(0)
    pl.semaphore_wait(barrier, 5 + BANDS - 1)
    begin(raws[0])
    group(1)
    begin(raws[1])
    group(2)
    a0.start()
    begin(raws[2])
    table(3)
    a0.wait()
    add_pair(0)
    begin(b0)
    orders_of(3)
    begin(raws[3])
    group(4)
    group(5)
    a1.start()
    finish(b0)
    add_four(0)
    c0.start()
    a1.wait()
    add_pair(1)
    begin(b1)
    basis()
    basis_copy = pltpu.make_async_copy(basis_v, basis_out, basis_sem)
    basis_copy.start()
    c0.wait()
    add_two(0)
    begin(d0)
    begin(raws[4])
    finish(d0)
    begin(f0)
    finish(b1)
    add_four(1)
    c1.start()
    c1.wait()
    add_two(1)
    begin(d1)
    begin(raws[5])
    begin(raws[6])
    finish(f0)
    g0.start()
    finish(d1)
    begin(f1)
    finish(raws[0])
    finish(raws[1])
    finish(raws[2])
    g0.wait()
    centre(0)
    finish(f1)
    g1.start()
    for copies in raws[3:]:
        finish(copies)
    g1.wait()
    centre(1)
    basis_copy.wait()
    for k in range(CHUNKS):
        for d in range(BANDS):
            outs(k, d).wait()


def fourier_blocks(coefficients):
    sem = pltpu.SemaphoreType.DMA
    bf = jnp.bfloat16
    basis = (BANDS * GROUPS * 2 * GO, LON)
    return pl.pallas_call(
        fourier_kernel,
        name="fourier_blocks",
        out_shape=[
            jax.ShapeDtypeStruct((BANDS, CHUNKS, PIECE, 128), bf),
            jax.ShapeDtypeStruct(basis, bf),
        ],
        in_specs=[pl.BlockSpec(memory_space=pl.ANY)],
        out_specs=[pl.BlockSpec(memory_space=pl.ANY)] * 2,
        scratch_shapes=[
            pltpu.VMEM((CH, ORDERS, 2, LP), jnp.int32),
            pltpu.VMEM((3, GO * MROWS, 128), jnp.float32),
            pltpu.VMEM((2, GO * LROWS, 128), jnp.float32),
            pltpu.VMEM((2, 384 * GO, 128), jnp.float32),
            pltpu.VMEM((BANDS * 48 * GO, 128), jnp.float32),
            pltpu.VMEM(basis, bf),
            pltpu.VMEM((CHUNKS, BANDS, PIECEP, 128), bf),
            pltpu.VMEM((CHUNKS, BANDS, PIECE, 128), bf),
            pltpu.VMEM((CHUNKS, BANDS, PIECEP, 128), bf),
            pltpu.VMEM((CHUNKS, BANDS, PIECEP // 2, 128), bf),
            pltpu.VMEM((CHUNKS, 3, BANDS, OWN, 128), bf),
            pltpu.VMEM((CHUNKS, BANDS, OWN, 128), bf),
            pltpu.VMEM((CHUNKS, BANDS, OWN, 128), bf),
            sem((GROUPS,)), sem((CHUNKS, BANDS)), sem,
            sem((7, 7)), sem((7, 7)),
            sem((2,)), sem((2,)),
            sem((2, 3)), sem((2, 3)),
            sem((2,)), sem((2,)),
            sem((2, 7)), sem((2, 7)),
            sem((2, 3)), sem((2, 3)),
            sem((2,)), sem((2,)),
        ],
        compiler_params=pltpu.CompilerParams(
            collective_id=1, has_side_effects=True, vmem_limit_bytes=63 * 2**20
        ),
    )(coefficients)


RB = 3


def synthesis_kernel(f_ref, basis_ref, scale_ref, weather_ref, out_ref):
    step = pl.program_id(0)
    rows = []
    for r in range(RB):
        x = f_ref[:, :, r].reshape(BANDS * GROUPS * 2 * GO, 128)
        rows.append(x.T)
    lhs = jnp.concatenate(rows, axis=0)
    noise = jnp.dot(lhs, basis_ref[...], preferred_element_type=jnp.float32)
    for r in range(RB):
        for q in range(Q):
            scale = scale_ref[q * R + step * RB + r]
            at = (r * Q + q) * 32
            out_ref[0, q, r] = (
                weather_ref[0, q, r].astype(jnp.float32) + scale * noise[at : at + 32]
            ).astype(jnp.bfloat16)


def synthesis(fourier, basis, scale, weather):
    fourier = fourier.reshape(BANDS, GROUPS, R, 2 * GO, 128)
    rows = weather.shape[2]
    weather = weather.reshape(1, Q, R, rows, LON)
    block = pl.BlockSpec((1, Q, RB, rows, LON), lambda i: (0, 0, i, 0, 0))
    out = pl.pallas_call(
        synthesis_kernel,
        name="synthesis",
        grid=(R // RB,),
        out_shape=jax.ShapeDtypeStruct(weather.shape, jnp.bfloat16),
        in_specs=[
            pl.BlockSpec((BANDS, GROUPS, RB, 2 * GO, 128), lambda i: (0, 0, i, 0, 0)),
            pl.BlockSpec(basis.shape, lambda i: (0, 0)),
            pl.BlockSpec(memory_space=pltpu.SMEM),
            block,
        ],
        out_specs=block,
        compiler_params=pltpu.CompilerParams(
            dimension_semantics=("arbitrary",), vmem_limit_bytes=63 * 2**20
        ),
    )(fourier, basis, scale, weather)
    return out.reshape(1, CH, rows, LON)


def local(weather, coefficients, channel_scale):
    centred, basis = fourier_blocks(coefficients.transpose(0, 1, 3, 2, 4))
    return synthesis(centred, basis, channel_scale, weather)


def solution(mesh):
    return jax.shard_map(
        local,
        mesh=mesh,
        in_specs=(P("member", None, "space", None), P("member", None, None, "space", None), P()),
        out_specs=P("member", None, "space", None),
        check_vma=False,
    )
```

time: 121 us -> 111 us (0.917)
  Pallas kernels: 116 us -> 110 us
  local copies, waits for them, and re-layouts: 2.83 us -> 0 us
  other arithmetic: 2.06 us -> 0 us
    pallas_call x1, Pallas kernels: 103 us -> 96.6 us  [fourier_blocks(): pl.pallas_call(fourier_kernel, name='fourier_blocks', out_shape=[jax.Shap...]
    unnamed x4 -> x0, local copies, waits for them, and re-layouts: 1.66 us -> none
where the time goes in v3:
time: 111 us; the launch traced here: 110 us
  Pallas kernels  110 us (99%)
    pallas_call x1, Pallas kernels, fourier_blocks(): pl.pallas_call(fourier_kernel, name='fourier_blocks', out_shape=[jax.Shap...  96.6 us
    pallas_call x1, Pallas kernels, synthesis(): pl.pallas_call(synthesis_kernel, name='synthesis', grid=(R // RB,), out_s...  13.5 us

profile of v3, /device:TPU:1, one launch (start us, length us, event | category | flops | bytes accessed | tf_op | source)
XLA Modules:
  0.0 110.1 jit_solution(5161554585225072292)
XLA Ops:
  0.0 96.6 %fourier_blocks.1 = (bf16[8,2,1008,128]{3,2,1,0:T(8,128)(2,1)}, bf16[768,1440]{1,0:T(8,128)(2,1)}) custom-call(s32[1,84,46,2,361]{4,3,2,1,0:T(2,128)} %bitcast.4), custom_call_target="tpu_custom_call" | custom-call | tf_op jit(solution)/shard_map/fourier_blocks/pallas_call | solution.py:480
  96.6 13.5 %synthesis.1 = bf16[1,4,21,32,1440]{4,3,2,1,0:T(8,128)(2,1)} custom-call(bf16[8,6,21,16,128]{4,3,2,1,0:T(8,128)(2,1)} %bitcast.6, bf16[768,1440]{1,0:T(8,128)(2,1)} %get-tuple-element.8.basis_ref, f32[84]{0:T(128)} %scale_ref.1, bf16[1,4,21,32,1440]{4,3,2,1,0:T(8,128)(2,1)} %bitcast.5), custom_call_target="tpu_custom_call" | custom-call | tf_op jit(solution)/shard_map/synthesis/pallas_call | solution.py:543

commit v4 on v3

--- a/solution.py
+++ b/solution.py
@@ -144,19 +144,13 @@
             degree = tile * 128 + lax.broadcasted_iota(jnp.int32, (GO, 128), 1)
             degree = degree.astype(jnp.float32)
             degree_square = degree * degree
-            prior = degree - 1.0
             up = jnp.sqrt(
                 jnp.maximum(4.0 * degree_square - 1.0, 1.0)
                 / jnp.maximum(degree_square - square, 1.0)
             )
-            down = up * jnp.sqrt(
-                jnp.maximum(prior * prior - square, 0.0)
-                / jnp.maximum(4.0 * prior * prior - 1.0, 1.0)
-            )
             for u in range(128):
                 row = pl.multiple_of((tile * 128 + u) * GO, 8)
-                factors[0, pl.ds(row, GO), :] = jnp.broadcast_to(up[:, u : u + 1], (GO, 128))
-                factors[1, pl.ds(row, GO), :] = jnp.broadcast_to(down[:, u : u + 1], (GO, 128))
+                factors[pl.ds(row, GO), :] = jnp.broadcast_to(up[:, u : u + 1], (GO, 128))
             return 0
 
         lax.fori_loop(0, 3, spread, 0)
@@ -164,29 +158,29 @@
         half_order = order_wide[:, :128]
 
         def block(j, carry, steps=8, channels=True):
-            older, newer = carry
+            older, newer, down = carry
             for u in range(steps):
                 deg = j * 8 + u
                 row = pl.multiple_of(deg * GO, 8)
-                up = factors[0, pl.ds(row, GO), :]
-                down = factors[1, pl.ds(row, GO), :]
+                up = factors[pl.ds(row, GO), :]
+                both = up * down
                 here = half_order == deg
                 fresh = []
                 for h in range(2):
                     at = slice(128 * h, 128 * h + 128)
                     seed = jnp.where(here, diag[:, at], 0.0)
-                    value = (up * cosine[:, at]) * newer[h] + (seed - down * older[h])
+                    value = (up * cosine[:, at]) * newer[h] + (seed - both * older[h])
                     tab[h, pl.ds(deg, 8, stride=LROWS), :] = value
                     fresh.append(value)
-                older, newer = newer, tuple(fresh)
+                older, newer, down = newer, tuple(fresh), 1.0 / up
                 if channels:
                     for i in (u % 4 * 2, u % 4 * 2 + 1):
                         if i < real(g):
                             arrange(g, j * 2 + u // 4, i)
-            return older, newer
+            return older, newer, down
 
         zero = jnp.zeros((GO, 128), jnp.float32)
-        carry = ((zero, zero), (zero, zero))
+        carry = ((zero, zero), (zero, zero), zero)
         carry = lax.fori_loop(0, CH // 2, block, carry)
         carry = lax.fori_loop(
             CH // 2, LP // 8, functools.partial(block, channels=False), carry
@@ -402,15 +396,11 @@
     d0, d1 = means_out(0), means_out(1)
     f0, f1 = z_gather(0), z_gather(1)
     g0, g1 = core_gather(0), core_gather(1)
-    raws = [
-        raw_group(0, 0),
-        raw_group(1, 1),
-        raw_group(2, 2),
-        raw_group(3, 3, 0, 176),
-        raw_group(4, 3, 176, GR - 176),
-        raw_group(5, 4),
-        raw_group(6, 5),
-    ]
+    pieces = (
+        (0, 0, GR), (1, 0, GR), (2, 0, GR), (3, 0, 224),
+        (3, 224, 64), (3, 288, 48), (4, 0, 64), (4, 64, 64), (4, 128, GR - 128), (5, 0, GR),
+    )
+    raws = [raw_group(n, *piece) for n, piece in enumerate(pieces)]
 
     group(0)
     pl.semaphore_wait(barrier, 5 + BANDS - 1)
@@ -432,30 +422,33 @@
     finish(b0)
     add_four(0)
     c0.start()
+    begin(raws[4])
     a1.wait()
     add_pair(1)
     begin(b1)
-    basis()
-    basis_copy = pltpu.make_async_copy(basis_v, basis_out, basis_sem)
-    basis_copy.start()
     c0.wait()
     add_two(0)
     begin(d0)
-    begin(raws[4])
+    begin(raws[5])
+    begin(raws[6])
     finish(d0)
     begin(f0)
     finish(b1)
     add_four(1)
     c1.start()
+    begin(raws[7])
     c1.wait()
     add_two(1)
     begin(d1)
-    begin(raws[5])
-    begin(raws[6])
+    begin(raws[8])
+    begin(raws[9])
     finish(f0)
     g0.start()
     finish(d1)
     begin(f1)
+    basis()
+    basis_copy = pltpu.make_async_copy(basis_v, basis_out, basis_sem)
+    basis_copy.start()
     finish(raws[0])
     finish(raws[1])
     finish(raws[2])
@@ -490,7 +483,7 @@
             pltpu.VMEM((CH, ORDERS, 2, LP), jnp.int32),
             pltpu.VMEM((3, GO * MROWS, 128), jnp.float32),
             pltpu.VMEM((2, GO * LROWS, 128), jnp.float32),
-            pltpu.VMEM((2, 384 * GO, 128), jnp.float32),
+            pltpu.VMEM((384 * GO, 128), jnp.float32),
             pltpu.VMEM((BANDS * 48 * GO, 128), jnp.float32),
             pltpu.VMEM(basis, bf),
             pltpu.VMEM((CHUNKS, BANDS, PIECEP, 128), bf),
@@ -501,7 +494,7 @@
             pltpu.VMEM((CHUNKS, BANDS, OWN, 128), bf),
             pltpu.VMEM((CHUNKS, BANDS, OWN, 128), bf),
             sem((GROUPS,)), sem((CHUNKS, BANDS)), sem,
-            sem((7, 7)), sem((7, 7)),
+            sem((10, 7)), sem((10, 7)),
             sem((2,)), sem((2,)),
             sem((2, 3)), sem((2, 3)),
             sem((2,)), sem((2,)),
@@ -515,7 +508,7 @@
     )(coefficients)
 
 
-RB = 3
+RB = 7
 
 
 def synthesis_kernel(f_ref, basis_ref, scale_ref, weather_ref, out_ref):

time: 111 us -> 103 us (0.928)
  Pallas kernels: 110 us -> 102 us
    pallas_call x1, Pallas kernels: 96.6 us -> 90 us  [fourier_blocks(): pl.pallas_call(fourier_kernel, name='fourier_blocks', out_shape=[jax.Shap...]
    pallas_call x1, Pallas kernels: 13.5 us -> 12.4 us  [synthesis(): pl.pallas_call(synthesis_kernel, name='synthesis', grid=(R // RB,), out_s...]
where the time goes in v4:
time: 103 us; the launch traced here: 102 us
  Pallas kernels  102 us (99%)
    pallas_call x1, Pallas kernels, fourier_blocks(): pl.pallas_call(fourier_kernel, name='fourier_blocks', out_shape=[jax.Shap...  90 us
    pallas_call x1, Pallas kernels, synthesis(): pl.pallas_call(synthesis_kernel, name='synthesis', grid=(R // RB,), out_s...  12.4 us

profile of v4, /device:TPU:1, one launch (start us, length us, event | category | flops | bytes accessed | tf_op | source)
XLA Modules:
  0.0 102.4 jit_solution(2252562641061683604)
XLA Ops:
  0.0 90.0 %fourier_blocks.1 = (bf16[8,2,1008,128]{3,2,1,0:T(8,128)(2,1)}, bf16[768,1440]{1,0:T(8,128)(2,1)}) custom-call(s32[1,84,46,2,361]{4,3,2,1,0:T(2,128)} %bitcast.4), custom_call_target="tpu_custom_call" | custom-call | tf_op jit(solution)/shard_map/fourier_blocks/pallas_call | solution.py:473
  90.0 12.4 %synthesis.1 = bf16[1,4,21,32,1440]{4,3,2,1,0:T(8,128)(2,1)} custom-call(bf16[8,6,21,16,128]{4,3,2,1,0:T(8,128)(2,1)} %bitcast.6, bf16[768,1440]{1,0:T(8,128)(2,1)} %get-tuple-element.8.basis_ref, f32[84]{0:T(128)} %scale_ref.1, bf16[1,4,21,32,1440]{4,3,2,1,0:T(8,128)(2,1)} %bitcast.5), custom_call_target="tpu_custom_call" | custom-call | tf_op jit(solution)/shard_map/synthesis/pallas_call | solution.py:536

commit v5 on v4

--- a/solution.py
+++ b/solution.py
@@ -51,7 +51,7 @@
 
 def fourier_kernel(
     coef_ref, out_ref, basis_out,
-    coef_v, lhs_v, tab, factors, stage, basis_v, f, got, mean, buf_a, buf_b, buf_c, piece,
+    coef_v, lhs_v, tab, factors, stage, basis_v, f, got, mean, buf_a, relay, buf_b, buf_c, piece,
     load_sem, out_sem, basis_sem,
     raw_s, raw_r, sa, ra, sb, rb, sc, rc, sd, rd, sf, rf, sg, rg,
 ):
@@ -75,12 +75,12 @@
     for load in loads:
         load.start()
 
-    z_peers = [member_of((z + d) % 4, xl, core) for d in (1, 2, 3)]
+    z_up, z_down = member_of((z + 1) % 4, xl, core), member_of((z + 3) % 4, xl, core)
     x_peer = member_of(z, 1 - xl, core)
     c_peer = member_of(z, xl, 1 - core)
     s_peers = [(space + d) % BANDS for d in range(1, BANDS)]
     barrier = pltpu.get_barrier_semaphore()
-    for peer in z_peers + [x_peer, c_peer]:
+    for peer in (z_up, z_down, x_peer, c_peer):
         pl.semaphore_signal(barrier, inc=1, device_id=(peer, space), device_id_type=MESH)
     for peer in s_peers:
         pl.semaphore_signal(barrier, inc=1, device_id=(member, peer), device_id_type=MESH)
@@ -258,14 +258,43 @@
         )
 
     def z_sums(k):
-        return [
-            remote(
-                buf_a.at[k, :, pl.ds(pl.multiple_of((z + d) % 4 * OWN, 16), OWN)],
-                buf_b.at[k, d - 1],
-                sb.at[k, d - 1], rb.at[k, d - 1], (z_peers[d - 1], space),
-            )
-            for d in (1, 2, 3)
+        def rows_of(place, at, size):
+            row = pl.multiple_of(place * OWN + at, 16)
+            return buf_a.at[k, :, pl.ds(row, size)]
+
+        far = (z + 2) % 4
+        first = [
+            remote(
+                rows_of(far, 0, OWN // 2), relay.at[k, 0], sb.at[k, 0], rb.at[k, 0],
+                (z_up, space),
+            ),
+            remote(
+                rows_of(far, OWN // 2, OWN // 2), relay.at[k, 1], sb.at[k, 1], rb.at[k, 1],
+                (z_down, space),
+            ),
         ]
+        second = [
+            remote(
+                rows_of((z + 1) % 4, 0, OWN), buf_b.at[k, 0], sb.at[k, 2], rb.at[k, 2],
+                (z_up, space),
+            ),
+            remote(
+                rows_of((z + 3) % 4, 0, OWN), buf_b.at[k, 1], sb.at[k, 3], rb.at[k, 3],
+                (z_down, space),
+            ),
+        ]
+        return first, second
+
+    def add_relay(k):
+        def one(s, _):
+            for n, place, at in ((0, (z + 1) % 4, 0), (1, (z + 3) % 4, OWN // 2)):
+                row = pl.multiple_of(place * OWN + at, 16)
+                total = buf_a[k, s, pl.ds(row, OWN // 2), :].astype(jnp.float32)
+                total += relay[k, n, s].astype(jnp.float32)
+                buf_a[k, s, pl.ds(row, OWN // 2), :] = total.astype(jnp.bfloat16)
+            return 0
+
+        lax.fori_loop(0, BANDS, one, 0)
 
     def x_sum(k):
         return remote(piece.at[k], buf_c.at[k], sc.at[k], rc.at[k], (x_peer, space))
@@ -280,13 +309,26 @@
         ]
 
     def z_gather(k):
-        return [
-            remote(
-                mean.at[k, :, pl.ds(own_row, OWN)], mean.at[k, :, pl.ds(own_row, OWN)],
-                sf.at[k, d - 1], rf.at[k, d - 1], (z_peers[d - 1], space),
-            )
-            for d in (1, 2, 3)
+        def rows_of(place, at, size):
+            row = pl.multiple_of(core * half + place * OWN + at, 16)
+            return mean.at[k, :, pl.ds(row, size)]
+
+        first = [
+            remote(rows_of(z, 0, OWN), rows_of(z, 0, OWN), sf.at[k, n], rf.at[k, n], device)
+            for n, device in enumerate(((z_up, space), (z_down, space)))
         ]
+        second = [
+            remote(
+                rows_of((z + 3) % 4, 0, OWN // 2), rows_of((z + 3) % 4, 0, OWN // 2),
+                sf.at[k, 2], rf.at[k, 2], (z_up, space),
+            ),
+            remote(
+                rows_of((z + 1) % 4, OWN // 2, OWN // 2),
+                rows_of((z + 1) % 4, OWN // 2, OWN // 2),
+                sf.at[k, 3], rf.at[k, 3], (z_down, space),
+            ),
+        ]
+        return first, second
 
     def core_gather(k):
         return remote(
@@ -325,7 +367,7 @@
     def add_four(k):
         def one(s, _):
             total = buf_a[k, s, pl.ds(in_half, OWN), :].astype(jnp.float32)
-            for d in range(3):
+            for d in range(2):
                 total += buf_b[k, d, s].astype(jnp.float32)
             piece[k, s] = total.astype(jnp.bfloat16)
             return 0
@@ -391,10 +433,10 @@
         return raw(g // PER, part, g % PER * GR + at, size)
 
     a0, a1 = pair_sum(0), pair_sum(1)
-    b0, b1 = z_sums(0), z_sums(1)
+    (r0, b0), (r1, b1) = z_sums(0), z_sums(1)
     c0, c1 = x_sum(0), x_sum(1)
     d0, d1 = means_out(0), means_out(1)
-    f0, f1 = z_gather(0), z_gather(1)
+    (f0, h0), (f1, h1) = z_gather(0), z_gather(1)
     g0, g1 = core_gather(0), core_gather(1)
     pieces = (
         (0, 0, GR), (1, 0, GR), (2, 0, GR), (3, 0, 224),
@@ -403,7 +445,7 @@
     raws = [raw_group(n, *piece) for n, piece in enumerate(pieces)]
 
     group(0)
-    pl.semaphore_wait(barrier, 5 + BANDS - 1)
+    pl.semaphore_wait(barrier, 4 + BANDS - 1)
     begin(raws[0])
     group(1)
     begin(raws[1])
@@ -413,8 +455,11 @@
     table(3)
     a0.wait()
     add_pair(0)
+    begin(r0)
+    orders_of(3)
+    finish(r0)
+    add_relay(0)
     begin(b0)
-    orders_of(3)
     begin(raws[3])
     group(4)
     group(5)
@@ -425,6 +470,9 @@
     begin(raws[4])
     a1.wait()
     add_pair(1)
+    begin(r1)
+    finish(r1)
+    add_relay(1)
     begin(b1)
     c0.wait()
     add_two(0)
@@ -437,15 +485,19 @@
     add_four(1)
     c1.start()
     begin(raws[7])
+    finish(f0)
+    begin(h0)
     c1.wait()
     add_two(1)
     begin(d1)
     begin(raws[8])
     begin(raws[9])
-    finish(f0)
+    finish(h0)
     g0.start()
     finish(d1)
     begin(f1)
+    finish(f1)
+    begin(h1)
     basis()
     basis_copy = pltpu.make_async_copy(basis_v, basis_out, basis_sem)
     basis_copy.start()
@@ -454,7 +506,7 @@
     finish(raws[2])
     g0.wait()
     centre(0)
-    finish(f1)
+    finish(h1)
     g1.start()
     for copies in raws[3:]:
         finish(copies)
@@ -490,16 +542,17 @@
             pltpu.VMEM((CHUNKS, BANDS, PIECE, 128), bf),
             pltpu.VMEM((CHUNKS, BANDS, PIECEP, 128), bf),
             pltpu.VMEM((CHUNKS, BANDS, PIECEP // 2, 128), bf),
-            pltpu.VMEM((CHUNKS, 3, BANDS, OWN, 128), bf),
+            pltpu.VMEM((CHUNKS, 2, BANDS, OWN // 2, 128), bf),
+            pltpu.VMEM((CHUNKS, 2, BANDS, OWN, 128), bf),
             pltpu.VMEM((CHUNKS, BANDS, OWN, 128), bf),
             pltpu.VMEM((CHUNKS, BANDS, OWN, 128), bf),
             sem((GROUPS,)), sem((CHUNKS, BANDS)), sem,
             sem((10, 7)), sem((10, 7)),
             sem((2,)), sem((2,)),
-            sem((2, 3)), sem((2, 3)),
+            sem((2, 4)), sem((2, 4)),
             sem((2,)), sem((2,)),
             sem((2, 7)), sem((2, 7)),
-            sem((2, 3)), sem((2, 3)),
+            sem((2, 4)), sem((2, 4)),
             sem((2,)), sem((2,)),
         ],
         compiler_params=pltpu.CompilerParams(

time: 103 us -> 111 us (1.078)
  Pallas kernels: 102 us -> 111 us
    pallas_call x1, Pallas kernels: 90 us -> 98.2 us  [fourier_blocks(): pl.pallas_call(fourier_kernel, name='fourier_blocks', out_shape=[jax.Shap...]
where the time goes in v5:
time: 111 us
  Pallas kernels  111 us (100%)
    pallas_call x1, Pallas kernels, fourier_blocks(): pl.pallas_call(fourier_kernel, name='fourier_blocks', out_shape=[jax.Shap...  98.2 us
    pallas_call x1, Pallas kernels, synthesis(): pl.pallas_call(synthesis_kernel, name='synthesis', grid=(R // RB,), out_s...  12.4 us

profile of v5, /device:TPU:1, one launch (start us, length us, event | category | flops | bytes accessed | tf_op | source)
XLA Modules:
  0.0 110.6 jit_solution(4596694873344624057)
XLA Ops:
  0.0 98.2 %fourier_blocks.1 = (bf16[8,2,1008,128]{3,2,1,0:T(8,128)(2,1)}, bf16[768,1440]{1,0:T(8,128)(2,1)}) custom-call(s32[1,84,46,2,361]{4,3,2,1,0:T(2,128)} %bitcast.4), custom_call_target="tpu_custom_call" | custom-call | tf_op jit(solution)/shard_map/fourier_blocks/pallas_call | solution.py:525
  98.2 12.4 %synthesis.1 = bf16[1,4,21,32,1440]{4,3,2,1,0:T(8,128)(2,1)} custom-call(bf16[8,6,21,16,128]{4,3,2,1,0:T(8,128)(2,1)} %bitcast.6, bf16[768,1440]{1,0:T(8,128)(2,1)} %get-tuple-element.8.basis_ref, f32[84]{0:T(128)} %scale_ref.1, bf16[1,4,21,32,1440]{4,3,2,1,0:T(8,128)(2,1)} %bitcast.5), custom_call_target="tpu_custom_call" | custom-call | tf_op jit(solution)/shard_map/synthesis/pallas_call | solution.py:589
